TPU v7x, 256 devices: a whole 4x4x8 slice. The times are simulated.
256 devices in a mesh: section: 16 (over z_lo, x), dp: 16 (over z_hi, y, core).
Axes of the slice: x: 4, y: 4, z: 8 (z_hi: 2, z_lo: 4; z = z_hi * 4 + z_lo), core: 2. Of those that a mesh axis runs over, the one named last changes fastest.
Arguments:
- carry_act: bfloat16 [16, 128, 2304], P('section', 'dp'), may hold values from -6 to 6
- carry_act_tan: bfloat16 [16, 128, 2304], P('section', 'dp'), may hold values from -6 to 6
- carry_adj: bfloat16 [16, 128, 2304], P('section', 'dp'), may hold values from -0.75 to 0.75
- carry_adj_tan: bfloat16 [16, 128, 2304], P('section', 'dp'), may hold values from -0.75 to 0.75
- fresh_act: bfloat16 [2, 128, 2304], P(None, 'dp'), may hold values from -6 to 6
- loss_cot: bfloat16 [2, 128, 2304], P(None, 'dp'), may hold values from -0.75 to 0.75
- stash_act: bfloat16 [16, 2, 128, 2304], P('section', None, 'dp'), may hold values from -6 to 6
- stash_act_tan: bfloat16 [16, 2, 128, 2304], P('section', None, 'dp'), may hold values from -6 to 6
- norm_gain: bfloat16 [16, 2304], P('section'), may hold values from 0.25 to 1.75
- up_weight: bfloat16 [16, 2304, 4608], P('section', None, 'dp'), may hold values from -0.125 to 0.125
- down_weight: bfloat16 [16, 4608, 2304], P('section', 'dp'), may hold values from -0.09375 to 0.09375
- up_dir: bfloat16 [16, 2304, 4608], P('section', None, 'dp'), may hold values from -0.125 to 0.125
- down_dir: bfloat16 [16, 4608, 2304], P('section', 'dp'), may hold values from -0.09375 to 0.09375
Outputs:
- next_act: bfloat16 [16, 128, 2304], P('section', 'dp')
- next_act_tan: bfloat16 [16, 128, 2304], P('section', 'dp')
- next_adj: bfloat16 [16, 128, 2304], P('section', 'dp')
- next_adj_tan: bfloat16 [16, 128, 2304], P('section', 'dp')
- hvp_up: bfloat16 [16, 2304, 4608], P('section', None, 'dp')
- hvp_down: bfloat16 [16, 4608, 2304], P('section', 'dp')
All inputs are finite; a program needn't handle non-finite values.
Results may differ from a plain program's by a relative error of at most 0.02.
Values may be sent and summed in bfloat16 or wider, within the bound.
A program may use at most 128 MiB of HBM per device.

v0:
```python
import jax
import jax.numpy as jnp
from jax import lax
from jax.sharding import PartitionSpec as P

TICKS = 2


sqrt_two_over_pi = 0.7978845608028654
cubic_coef = 0.044715
norm_eps = 1e-06


def in_one_piece(arrays, axis, dim, along):
    both = jnp.concatenate(arrays, axis=along)
    whole, at, done = (lax.all_gather(both, axis, axis=dim, tiled=True), 0, [])
    for a in arrays:
        done.append(lax.slice_in_dim(whole, at, at + a.shape[along], axis=along))
        at += a.shape[along]
    return tuple(done)


def split_up(value, dim, length):
    shape = value.shape
    parts = value.reshape(*shape[:dim], length, shape[dim] // length, *shape[dim + 1 :])
    return jnp.moveaxis(parts, dim, 0)


def one_scatter(arrays, axis, dims):
    length = lax.axis_size(axis)
    parts = [split_up(a, dim, length) for a, dim in zip(arrays, dims)]
    lines = jnp.concatenate([b.reshape(length, -1) for b in parts], axis=1)
    rows = max(16, -(-lines.shape[1] // 1024) * 8)
    lines = jnp.pad(lines, ((0, 0), (0, rows * 128 - lines.shape[1]))).reshape(-1, 128)
    line, at, done = (lax.psum_scatter(lines, axis, tiled=True).reshape(-1), 0, [])
    for b in parts:
        part = b[0]
        done.append(line[at : at + part.size].reshape(part.shape))
        at += part.size
    return tuple(done)


def passed_along(value, axis, steps):
    count = lax.axis_size(axis)
    leading, last = (max(0, -steps), min(count, count - steps))
    return lax.ppermute(value, axis, [(source, source + steps) for source in range(leading, last)])


def gelu_parts(linear):
    inner_arg = sqrt_two_over_pi * (linear + cubic_coef * linear * linear * linear)
    first_slope = sqrt_two_over_pi * (1.0 + 3.0 * cubic_coef * linear * linear)
    second_slope = 6.0 * sqrt_two_over_pi * cubic_coef * linear
    tanh_value = jnp.tanh(inner_arg)
    sech_square = 1.0 - tanh_value * tanh_value
    gelu_value = 0.5 * linear * (1.0 + tanh_value)
    gelu_first = 0.5 * (1.0 + tanh_value) + 0.5 * linear * sech_square * first_slope
    gelu_second = sech_square * (
        first_slope - linear * tanh_value * first_slope * first_slope + 0.5 * linear * second_slope
    )
    return (gelu_value, gelu_first, gelu_second)


def matrix_product(left, right):
    return jnp.dot(left, right, preferred_element_type=jnp.float32)


def product_last(left, right):
    return lax.dot_general(
        left, right, (((1,), (1,)), ((), ())), preferred_element_type=jnp.float32
    )


def product_first(left, right):
    return lax.dot_general(
        left, right, (((0,), (0,)), ((), ())), preferred_element_type=jnp.float32
    )


def norm_stats(rows, rows_tan):
    values = rows.astype(jnp.float32)
    values_tan = rows_tan.astype(jnp.float32)
    inverse = lax.rsqrt(jnp.mean(values * values, axis=-1, keepdims=True) + norm_eps)
    inverse_tan = -(inverse * inverse * inverse) * jnp.mean(
        values * values_tan, axis=-1, keepdims=True
    )
    return (values, values_tan, inverse, inverse_tan)


def norm_rows(rows, rows_tan, gain_row):
    values, values_tan, inverse, inverse_tan = norm_stats(rows, rows_tan)
    gain_wide = gain_row.astype(jnp.float32)
    normed = (values * inverse * gain_wide).astype(jnp.bfloat16)
    normed_tan = ((values_tan * inverse + values * inverse_tan) * gain_wide).astype(jnp.bfloat16)
    return (normed, normed_tan)


def norm_back(rows, rows_tan, gain_row, arriving, arriving_tan, summed, summed_tan):
    values, values_tan, inverse, inverse_tan = norm_stats(rows, rows_tan)
    gain_wide = gain_row.astype(jnp.float32)
    weighted = summed * gain_wide
    weighted_tan = summed_tan * gain_wide
    moment = jnp.mean(values * weighted, axis=-1, keepdims=True)
    moment_tan = jnp.mean(values_tan * weighted + values * weighted_tan, axis=-1, keepdims=True)
    inverse_cube = inverse * inverse * inverse
    returned = arriving.astype(jnp.float32) + inverse * weighted - inverse_cube * values * moment
    returned_tan = (
        arriving_tan.astype(jnp.float32)
        + inverse_tan * weighted
        + inverse * weighted_tan
        - 3.0 * inverse * inverse * inverse_tan * values * moment
        - inverse_cube * values_tan * moment
        - inverse_cube * values * moment_tan
    )
    return (returned.astype(jnp.bfloat16), returned_tan.astype(jnp.bfloat16))


def branch_forward(normed, normed_tan, up_local, down_local, up_direction, down_direction):
    linear = matrix_product(normed, up_local)
    linear_tan = matrix_product(normed_tan, up_local) + matrix_product(normed, up_direction)
    gelu_value, gelu_first, gelu_second = gelu_parts(linear)
    hidden = gelu_value.astype(jnp.bfloat16)
    hidden_tan = (gelu_first * linear_tan).astype(jnp.bfloat16)
    partial_value = matrix_product(hidden, down_local)
    partial_tan = matrix_product(hidden_tan, down_local) + matrix_product(hidden, down_direction)
    return (partial_value, partial_tan)


def branch_backward(
    stash_normed,
    stash_normed_tan,
    adjoint_all,
    adjoint_all_tan,
    up_local,
    down_local,
    up_direction,
    down_direction,
):
    linear = matrix_product(stash_normed, up_local)
    linear_tan = matrix_product(stash_normed_tan, up_local) + matrix_product(
        stash_normed, up_direction
    )
    gelu_value, gelu_first, gelu_second = gelu_parts(linear)
    hidden = gelu_value.astype(jnp.bfloat16)
    hidden_tan = (gelu_first * linear_tan).astype(jnp.bfloat16)
    upstream = product_last(adjoint_all, down_local)
    upstream_tan = product_last(adjoint_all_tan, down_local) + product_last(
        adjoint_all, down_direction
    )
    deltas = (upstream * gelu_first).astype(jnp.bfloat16)
    deltas_tan = (upstream_tan * gelu_first + upstream * gelu_second * linear_tan).astype(
        jnp.bfloat16
    )
    curvature_down = product_first(hidden_tan, adjoint_all) + product_first(hidden, adjoint_all_tan)
    curvature_up = product_first(stash_normed_tan, deltas) + product_first(stash_normed, deltas_tan)
    partial_value = product_last(deltas, up_local)
    partial_tan = product_last(deltas_tan, up_local) + product_last(deltas, up_direction)
    return (partial_value, partial_tan, curvature_up, curvature_down)


def gather_rows(lead_rows, lead_tan, stash_rows, stash_tan, adjoint_rows, adjoint_tan):
    joined = in_one_piece(
        (lead_rows, lead_tan, stash_rows, stash_tan, adjoint_rows, adjoint_tan), "dp", 0, 1
    )
    return ((joined[0], joined[1]), (joined[2], joined[3], joined[4], joined[5]))


def reduce_rows(forward_term, forward_tan, backward_term, backward_tan):
    joined = tuple(
        (
            part.astype(jnp.float32)
            for part in one_scatter(
                (
                    forward_term.astype(jnp.bfloat16),
                    forward_tan.astype(jnp.bfloat16),
                    backward_term.astype(jnp.bfloat16),
                    backward_tan.astype(jnp.bfloat16),
                ),
                "dp",
                (0, 0, 0, 0),
            )
        )
    )
    return ((joined[0], joined[1]), (joined[2], joined[3]))


def shards(
    carry_act,
    carry_act_tan,
    carry_adj,
    carry_adj_tan,
    fresh_act,
    loss_cot,
    stash_act,
    stash_act_tan,
    norm_gain,
    up_weight,
    down_weight,
    up_dir,
    down_dir,
):
    section_index = lax.axis_index("section")
    section_count = lax.axis_size("section")
    at_first = section_index == 0
    at_last = section_index == section_count - 1
    gain_row = norm_gain[0]
    up_local = up_weight[0]
    down_local = down_weight[0]
    up_direction = up_dir[0]
    down_direction = down_dir[0]
    activation, activation_tan = (carry_act[0], carry_act_tan[0])
    adjoint, adjoint_tan = (carry_adj[0], carry_adj_tan[0])
    total_up = jnp.zeros(up_local.shape, jnp.float32)
    total_down = jnp.zeros(down_local.shape, jnp.float32)
    for tick_index in range(TICKS):
        fresh_rows = fresh_act[tick_index]
        cotangent = loss_cot[tick_index]
        zero_rows = jnp.zeros_like(fresh_rows)
        stash_rows = stash_act[0, tick_index]
        stash_tan = stash_act_tan[0, tick_index]
        moved_forward = passed_along((activation, activation_tan), "section", 1)
        moved_backward = passed_along((adjoint, adjoint_tan), "section", -1)
        input_rows = jnp.where(at_first, fresh_rows, moved_forward[0])
        input_tan = jnp.where(at_first, zero_rows, moved_forward[1])
        arriving = jnp.where(at_last, cotangent, moved_backward[0])
        arriving_tan = jnp.where(at_last, zero_rows, moved_backward[1])
        normed, normed_tan = norm_rows(input_rows, input_tan, gain_row)
        stash_normed, stash_normed_tan = norm_rows(stash_rows, stash_tan, gain_row)
        forward_rows, backward_rows = gather_rows(
            normed, normed_tan, stash_normed, stash_normed_tan, arriving, arriving_tan
        )
        normed_all, normed_all_tan = (forward_rows[0], forward_rows[1])
        stash_all, stash_all_tan = (backward_rows[0], backward_rows[1])
        adjoint_all, adjoint_all_tan = (backward_rows[2], backward_rows[3])
        partial_value, partial_tan = branch_forward(
            normed_all, normed_all_tan, up_local, down_local, up_direction, down_direction
        )
        back_partial, back_partial_tan, curvature_up, curvature_down = branch_backward(
            stash_all,
            stash_all_tan,
            adjoint_all,
            adjoint_all_tan,
            up_local,
            down_local,
            up_direction,
            down_direction,
        )
        summed_forward, summed_backward = reduce_rows(
            partial_value, partial_tan, back_partial, back_partial_tan
        )
        total_up = total_up + curvature_up
        total_down = total_down + curvature_down
        activation = (input_rows.astype(jnp.float32) + summed_forward[0]).astype(jnp.bfloat16)
        activation_tan = (input_tan.astype(jnp.float32) + summed_forward[1]).astype(jnp.bfloat16)
        adjoint, adjoint_tan = norm_back(
            stash_rows,
            stash_tan,
            gain_row,
            arriving,
            arriving_tan,
            summed_backward[0],
            summed_backward[1],
        )
    return (
        activation[None],
        activation_tan[None],
        adjoint[None],
        adjoint_tan[None],
        total_up.astype(jnp.bfloat16)[None],
        total_down.astype(jnp.bfloat16)[None],
    )


def solution(mesh):
    in_specs = (
        P("section", "dp", None),
        P("section", "dp", None),
        P("section", "dp", None),
        P("section", "dp", None),
        P(None, "dp", None),
        P(None, "dp", None),
        P("section", None, "dp", None),
        P("section", None, "dp", None),
        P("section", None),
        P("section", None, "dp"),
        P("section", "dp", None),
        P("section", None, "dp"),
        P("section", "dp", None),
    )
    out_specs = (
        P("section", "dp", None),
        P("section", "dp", None),
        P("section", "dp", None),
        P("section", "dp", None),
        P("section", None, "dp"),
        P("section", "dp", None),
    )
    return jax.shard_map(shards, mesh=mesh, in_specs=in_specs, out_specs=out_specs, check_vma=False)
```

profile of v0, /device:TPU:32, one launch (start us, length us, event | category | flops | bytes accessed | tf_op | source)
XLA Modules:
  0.0 448.3 jit_solution(13519780258735777881)
XLA Ops:
  7.2 3.5 collective-permute-start.1
  10.8 3.4 collective-permute-start
  14.2 4.6 %collective-permute-start.2 = (bf16[8,2304]{1,0:T(8,128)(2,1)}, bf16[8,2304]{1,0:T(8,128)(2,1)S(1)}, u32[]{:S(2)}, u32[]{:S(2)}) collective-permute-start(bf16[8,2304]{1,0:T(8,128)(2,1)} %bitcast.186), channel_id=1, source_target_pairs={{16,0},{32,16},{48,32},{64,48},{80,64},{96,80},{112,96},{128,112},... | collective-permute-start | bytes 110600 | tf_op jit(solution)/shard_map/ppermute | solution.py:46
  18.7 2.4 collective-permute-start.3
  28.5 72.7 %all-gather.3.cloned.1.call-done = bf16[128,13824]{1,0:T(8,128)(2,1)} async-done(((bf16[8,13824]{1,0:T(8,128)(2,1)}), bf16[128,13824]{1,0:T(8,128)(2,1)}) %all-gather.3.cloned.1.call-update) | async-done | bytes 3538960 | tf_op jit(solution)/shard_map/all_gather | solution.py:16
  102.8 2.8 convolution_convert_fusion.3
  107.2 3.7 fusion.37
  110.9 3.0 fusion.6
  128.3 2.1 reshape_reshape.27
  130.4 2.1 reshape_reshape.26
  132.6 2.1 reshape_reshape.24
  134.7 3.0 pad_maximum_fusion
  137.7 3.5 reshape.196
  141.3 84.8 %reduce-scatter.3.cloned.1.call-done = bf16[576,128]{1,0:T(8,128)(2,1)} async-done(((bf16[9216,128]{1,0:T(8,128)(2,1)}), bf16[576,128]{1,0:T(8,128)(2,1)}) %reduce-scatter.3.cloned.1.call-update) | async-done | bytes 147472 | tf_op jit(solution)/shard_map/reduce_scatter | solution.py:35
  229.1 6.4 %collective-permute-start.6 = (bf16[8,2304]{1,0:T(8,128)(2,1)}, bf16[8,2304]{1,0:T(8,128)(2,1)S(1)}, u32[]{:S(2)}, u32[]{:S(2)}) collective-permute-start(bf16[8,2304]{1,0:T(8,128)(2,1)} %get-tuple-element.27), channel_id=1, source_target_pairs={{16,0},{32,16},{48,32},{64,48},{80,64},{96,80},{112,96},{128,112},... | collective-permute-start | bytes 110600 | tf_op jit(solution)/shard_map/ppermute | solution.py:46
  235.6 1.9 collective-permute-start.4
  239.5 6.0 %collective-permute-start.7 = (bf16[8,2304]{1,0:T(8,128)(2,1)S(1)}, bf16[8,2304]{1,0:T(8,128)(2,1)S(1)}, u32[]{:S(2)}, u32[]{:S(2)}) collective-permute-start(bf16[8,2304]{1,0:T(8,128)(2,1)S(1)} %get-tuple-element.26), channel_id=1, source_target_pairs={{16,0},{32,16},{48,32},{64,48},{80,64},{96,80},{112,96},{128,112},... | collective-permute-start | bytes 110600 | tf_op jit(solution)/shard_map/ppermute | solution.py:46
  249.2 67.9 %all-gather.5.cloned.1.call-done = bf16[128,13824]{1,0:T(8,128)(2,1)} async-done(((bf16[8,13824]{1,0:T(8,128)(2,1)}), bf16[128,13824]{1,0:T(8,128)(2,1)}) %all-gather.5.cloned.1.call-update) | async-done | bytes 3538960 | tf_op jit(solution)/shard_map/all_gather | solution.py:16
  321.7 3.7 fusion.30
  325.5 3.0 fusion.8
  345.5 2.1 reshape_reshape.28
  347.7 2.6 pad_maximum_fusion.1
  350.3 3.4 reshape.197
  366.7 72.0 %reduce-scatter.5.cloned.1.call-done = bf16[576,128]{1,0:T(8,128)(2,1)} async-done(((bf16[9216,128]{1,0:T(8,128)(2,1)}), bf16[576,128]{1,0:T(8,128)(2,1)}) %reduce-scatter.5.cloned.1.call-update) | async-done | bytes 147472 | tf_op jit(solution)/shard_map/reduce_scatter | solution.py:35
  (191 shorter events, 70.7 us)
Async XLA Ops:
  7.2 94.0 %copy-start = (bf16[1,2304,288]{1,2,0:T(8,128)(2,1)S(1)}, bf16[1,2304,288]{1,2,0:T(8,128)(2,1)}, u32[]{:S(2)}) copy-start(bf16[1,2304,288]{1,2,0:T(8,128)(2,1)} %param.22) | copy-start | bytes 3981316
  7.2 94.0 %all-gather.3.cloned.1.call-start = ((), (), s32[]{:S(2)}) async-start(), calls=%async_computation.2 | async-start | bytes 3760128 | tf_op jit(solution)/shard_map/all_gather | solution.py:16
  7.2 16.3 %collective-permute-start.1 = (bf16[8,2304]{1,0:T(8,128)(2,1)}, bf16[8,2304]{1,0:T(8,128)(2,1)S(1)}, u32[]{:S(2)}, u32[]{:S(2)}) collective-permute-start(bf16[8,2304]{1,0:T(8,128)(2,1)} %bitcast.184), channel_id=1, source_target_pairs={{0,16},{16,32},{32,48},{48,64},{64,80},{80,96},{96,112},{112,128},... | collective-permute-start | bytes 110600 | tf_op jit(solution)/shard_map/ppermute | solution.py:46
  10.8 12.7 %collective-permute-start = (bf16[8,2304]{1,0:T(8,128)(2,1)}, bf16[8,2304]{1,0:T(8,128)(2,1)S(1)}, u32[]{:S(2)}, u32[]{:S(2)}) collective-permute-start(bf16[8,2304]{1,0:T(8,128)(2,1)} %bitcast.185), channel_id=1, source_target_pairs={{0,16},{16,32},{32,48},{48,64},{64,80},{80,96},{96,112},{112,128},... | collective-permute-start | bytes 110600 | tf_op jit(solution)/shard_map/ppermute | solution.py:46
  14.2 12.7 %collective-permute-start.2 = (bf16[8,2304]{1,0:T(8,128)(2,1)}, bf16[8,2304]{1,0:T(8,128)(2,1)S(1)}, u32[]{:S(2)}, u32[]{:S(2)}) collective-permute-start(bf16[8,2304]{1,0:T(8,128)(2,1)} %bitcast.186), channel_id=1, source_target_pairs={{16,0},{32,16},{48,32},{64,48},{80,64},{96,80},{112,96},{128,112},... | collective-permute-start | bytes 110600 | tf_op jit(solution)/shard_map/ppermute | solution.py:46
  18.7 9.0 %collective-permute-start.3 = (bf16[8,2304]{1,0:T(8,128)(2,1)}, bf16[8,2304]{1,0:T(8,128)(2,1)S(1)}, u32[]{:S(2)}, u32[]{:S(2)}) collective-permute-start(bf16[8,2304]{1,0:T(8,128)(2,1)} %bitcast.187), channel_id=1, source_target_pairs={{16,0},{32,16},{48,32},{64,48},{80,64},{96,80},{112,96},{128,112},... | collective-permute-start | bytes 110600 | tf_op jit(solution)/shard_map/ppermute | solution.py:46
  22.7 80.0 %copy-start.46 = (f32[8]{0:T(128)}, f32[8]{0:T(128)S(1)}, u32[]{:S(2)}) copy-start(f32[8]{0:T(128)S(1)} %get-tuple-element.21) | copy-start | bytes 100
  23.5 77.7 %copy-start.24 = (bf16[8,2304]{1,0:T(8,128)(2,1)}, bf16[8,2304]{1,0:T(8,128)(2,1)S(1)}, u32[]{:S(2)}) copy-start(bf16[8,2304]{1,0:T(8,128)(2,1)S(1)} %collective-permute-done.1) | copy-start | bytes 110596
  28.5 197.6 %reduce-scatter.3.cloned.1.call-start = ((), (), s32[]{:S(2)}) async-start(), calls=%async_computation.3 | async-start | bytes 2506752 | tf_op jit(solution)/shard_map/reduce_scatter | solution.py:35
  141.2 85.8 %copy-start.8 = (bf16[1,2,8,2304]{3,2,1,0:T(8,128)(2,1)S(1)}, bf16[1,2,8,2304]{3,2,1,0:T(8,128)(2,1)}, u32[]{:S(2)}) copy-start(bf16[1,2,8,2304]{3,2,1,0:T(8,128)(2,1)} %param.19) | copy-start | bytes 221188
  141.2 85.8 %copy-start.11 = (bf16[1,2,8,2304]{3,2,1,0:T(8,128)(2,1)S(1)}, bf16[1,2,8,2304]{3,2,1,0:T(8,128)(2,1)}, u32[]{:S(2)}) copy-start(bf16[1,2,8,2304]{3,2,1,0:T(8,128)(2,1)} %param.20) | copy-start | bytes 221188
  141.2 86.5 %copy-start.34 = (bf16[2,8,2304]{2,1,0:T(8,128)(2,1)S(1)}, bf16[2,8,2304]{2,1,0:T(8,128)(2,1)}, u32[]{:S(2)}) copy-start(bf16[2,8,2304]{2,1,0:T(8,128)(2,1)} %param.18) | copy-start | bytes 221188
  141.2 86.5 %copy-start.39 = (bf16[8,2304]{1,0:T(8,128)(2,1)S(1)}, bf16[8,2304]{1,0:T(8,128)(2,1)}, u32[]{:S(2)}) copy-start(bf16[8,2304]{1,0:T(8,128)(2,1)} %copy-done.38) | copy-start | bytes 110596
  141.2 86.5 %copy-start.43 = (bf16[8,2304]{1,0:T(8,128)(2,1)S(1)}, bf16[8,2304]{1,0:T(8,128)(2,1)}, u32[]{:S(2)}) copy-start(bf16[8,2304]{1,0:T(8,128)(2,1)} %copy-done.42) | copy-start | bytes 110596
  141.2 94.4 %copy-start.21 = (bf16[8,2304]{1,0:T(8,128)(2,1)S(1)}, bf16[8,2304]{1,0:T(8,128)(2,1)}, u32[]{:S(2)}) copy-start(bf16[8,2304]{1,0:T(8,128)(2,1)} %copy-done.20) | copy-start | bytes 110596
  141.2 96.3 %copy-start.25 = (bf16[8,2304]{1,0:T(8,128)(2,1)S(1)}, bf16[8,2304]{1,0:T(8,128)(2,1)}, u32[]{:S(2)}) copy-start(bf16[8,2304]{1,0:T(8,128)(2,1)} %copy-done.24) | copy-start | bytes 110596
  141.2 175.9 %all-gather.5.cloned.1.call-start = ((), (), s32[]{:S(2)}) async-start(), calls=%async_computation.4 | async-start | bytes 3760128 | tf_op jit(solution)/shard_map/all_gather | solution.py:16
  229.1 19.0 %collective-permute-start.6 = (bf16[8,2304]{1,0:T(8,128)(2,1)}, bf16[8,2304]{1,0:T(8,128)(2,1)S(1)}, u32[]{:S(2)}, u32[]{:S(2)}) collective-permute-start(bf16[8,2304]{1,0:T(8,128)(2,1)} %get-tuple-element.27), channel_id=1, source_target_pairs={{16,0},{32,16},{48,32},{64,48},{80,64},{96,80},{112,96},{128,112},... | collective-permute-start | bytes 110600 | tf_op jit(solution)/shard_map/ppermute | solution.py:46
  235.6 11.2 %collective-permute-start.4 = (bf16[8,2304]{1,0:T(8,128)(2,1)S(1)}, bf16[8,2304]{1,0:T(8,128)(2,1)S(1)}, u32[]{:S(2)}, u32[]{:S(2)}) collective-permute-start(bf16[8,2304]{1,0:T(8,128)(2,1)S(1)} %fusion.228), channel_id=1, source_target_pairs={{0,16},{16,32},{32,48},{48,64},{64,80},{80,96},{96,112},{112,128},... | collective-permute-start | bytes 110600 | tf_op jit(solution)/shard_map/ppermute | solution.py:46
  237.6 9.3 %collective-permute-start.5 = (bf16[8,2304]{1,0:T(8,128)(2,1)S(1)}, bf16[8,2304]{1,0:T(8,128)(2,1)S(1)}, u32[]{:S(2)}, u32[]{:S(2)}) collective-permute-start(bf16[8,2304]{1,0:T(8,128)(2,1)S(1)} %fusion.205), channel_id=1, source_target_pairs={{0,16},{16,32},{32,48},{48,64},{64,80},{80,96},{96,112},{112,128},... | collective-permute-start | bytes 110600 | tf_op jit(solution)/shard_map/ppermute | solution.py:46
  239.5 8.7 %collective-permute-start.7 = (bf16[8,2304]{1,0:T(8,128)(2,1)S(1)}, bf16[8,2304]{1,0:T(8,128)(2,1)S(1)}, u32[]{:S(2)}, u32[]{:S(2)}) collective-permute-start(bf16[8,2304]{1,0:T(8,128)(2,1)S(1)} %get-tuple-element.26), channel_id=1, source_target_pairs={{16,0},{32,16},{48,32},{64,48},{80,64},{96,80},{112,96},{128,112},... | collective-permute-start | bytes 110600 | tf_op jit(solution)/shard_map/ppermute | solution.py:46
  249.0 189.7 %reduce-scatter.5.cloned.1.call-start = ((), (), s32[]{:S(2)}) async-start(), calls=%async_computation.5 | async-start | bytes 2506752 | tf_op jit(solution)/shard_map/reduce_scatter | solution.py:35
  365.0 74.7 %copy-start.19 = (bf16[8,2304]{1,0:T(8,128)(2,1)S(1)}, bf16[8,2304]{1,0:T(8,128)(2,1)}, u32[]{:S(2)}) copy-start(bf16[8,2304]{1,0:T(8,128)(2,1)} %copy-done.18) | copy-start | bytes 110596
  366.6 74.4 %copy-start.41 = (bf16[8,2304]{1,0:T(8,128)(2,1)S(1)}, bf16[8,2304]{1,0:T(8,128)(2,1)}, u32[]{:S(2)}) copy-start(bf16[8,2304]{1,0:T(8,128)(2,1)} %copy-done.40) | copy-start | bytes 110596
  (37 other events, 862.3 us)
Sparse Core Ops, SparseCore 0:
  28.6 72.5 all-gather.2
  141.3 84.7 reduce-scatter.2
  249.1 67.9 all-gather.4
  353.8 84.7 reduce-scatter.4
where the time goes:
time: 453 us; the launch traced here: 448 us
  waiting for transfers between devices  297 us (66%)
  matrix products  60.4 us (13%)
  starting transfers between devices  30.6 us (7%)
  local copies, waits for them, and re-layouts  25.1 us (6%)
  other arithmetic  20.1 us (4%)
  between operations  14.7 us (3%)
    reduce_scatter x2, waiting for transfers between devices, one_scatter(): lax.psum_scatter(lines, axis, tiled=True).reshape(-1)  157 us
    all_gather x2, waiting for transfers between devices, in_one_piece(): whole, at, done = (lax.all_gather(both, axis, axis=dim, tiled=True), 0, [])  141 us
    dot_general x16, matrix products, matrix_product(): return jnp.dot(left, right, preferred_element_type=jnp.float32)  33.7 us
    ppermute x8, starting transfers between devices, passed_along(): lax.ppermute(value, axis, [(source, source + steps) for source in range(l...  30.2 us
    dot_general x12, matrix products, product_last(): lax.dot_general(left, right, (((1,), (1,)), ((), ())), preferred_element_...  16 us
    another operation x8, local copies, waits for them, and re-layouts, one_scatter(): lines = jnp.concatenate([b.reshape(length, -1) for b in parts], axis=1)  13.9 us
    dot_general x8, matrix products, product_first(): lax.dot_general(left, right, (((0,), (0,)), ((), ())), preferred_element_...  10.7 us
  transfers between devices with their start and end apart: 12, of which 4 were waited for; matrix products, arithmetic and copies ran while one was open for 4% of the time, Pallas kernels for 0%

commit v1 on v0

v1 whole, which is shorter than its diff:
```python
import jax
import jax.numpy as jnp
from jax import lax
from jax.experimental import pallas as pl
from jax.experimental.pallas import tpu as pltpu
from jax.sharding import PartitionSpec as P

MESH = pl.DeviceIdType.MESH
F32, BF16 = jnp.float32, jnp.bfloat16

ROOT = 0.7978845608028654
CUBIC = 0.044715
EPS = 1e-06

D = 2304
W = 288
WP = 384
NC = 3
CW = D // NC
M1, A1, N1, M2, A2, N2 = range(6)
T1, P1, T2, P2 = range(4)


def gelu_parts(v):
    u = ROOT * (v + CUBIC * v * v * v)
    s1 = ROOT * (1.0 + 3.0 * CUBIC * v * v)
    s2 = 6.0 * ROOT * CUBIC * v
    th = jnp.tanh(u)
    sech = 1.0 - th * th
    g0 = 0.5 * v * (1.0 + th)
    g1 = 0.5 * (1.0 + th) + 0.5 * v * sech * s1
    g2 = sech * (s1 - v * th * s1 * s1 + 0.5 * v * s2)
    return g0, g1, g2


def stats(r, rt):
    inv = lax.rsqrt(jnp.mean(r * r, axis=-1, keepdims=True) + EPS)
    inv_t = -(inv * inv * inv) * jnp.mean(r * rt, axis=-1, keepdims=True)
    return inv, inv_t


def norm_pair(block, gain):
    r, rt = block[:8], block[8:]
    inv, inv_t = stats(r, rt)
    return jnp.concatenate([r * inv * gain, (rt * inv + r * inv_t) * gain], axis=0).astype(BF16)


def norm_back(block, arriving, grads, gain):
    x, xt = block[:8], block[8:]
    inv, inv_t = stats(x, xt)
    w, wt = grads[:8] * gain, grads[8:] * gain
    mu = jnp.mean(x * w, axis=-1, keepdims=True)
    mu_t = jnp.mean(xt * w + x * wt, axis=-1, keepdims=True)
    cube = inv * inv * inv
    out = arriving[:8] + inv * w - cube * x * mu
    out_t = (
        arriving[8:]
        + inv_t * w
        + inv * wt
        - 3.0 * inv * inv * inv_t * x * mu
        - cube * xt * mu
        - cube * x * mu_t
    )
    return out, out_t


def kernel(
    c_act, c_act_t, c_adj, c_adj_t, fresh, loss, stash, stash_t, gain_ref, up_h, down_h, upd_h, downd_h,
    o_act, o_act_t, o_adj, o_adj_t, o_up, o_down,
    G, ST, IN, CA, SH, WU, WV, AB, XT, XP, QC, ZC, OWN, PS, PR, YS, YR, ZS, ZR, FB, CU, CD, CO,
    w_sem, o_sem, lane_r, lane_s, part_r, part_s, pr_r, pr_s, yr_r, yr_s, zr_r, zr_s, in_r, in_s, ad_r, ad_s, st_r, st_s,
):
    s, d = lax.axis_index("section"), lax.axis_index("dp")
    z, y, c = lax.div(d, 8), lax.rem(lax.div(d, 2), 4), lax.rem(d, 2)
    zo, co = 1 - z, 1 - c
    s_up, s_dn = lax.rem(s + 1, 16), lax.rem(s + 15, 16)

    def dev(ss, zz, yy, cc):
        return (ss, zz * 8 + yy * 2 + cc)

    def slot(cc, yy, zz):
        return cc * 8 + yy * 2 + zz

    ynb = [y, lax.rem(y + 1, 4), lax.rem(y + 2, 4), lax.rem(y + 3, 4)]
    ysrc = [y, ynb[3], ynb[2], ynb[1]]
    partner = dev(s, z, y, co)
    across = dev(s, zo, y, c)
    own = [slot(c, y, z), slot(c, y, zo)]
    zhs = [z, zo]

    loads = []
    for i, (src, dst) in enumerate(((up_h, WU.at[pl.ds(0, W)]), (upd_h, WU.at[pl.ds(WP, W)]),
                                    (down_h, WV.at[pl.ds(0, W)]), (downd_h, WV.at[pl.ds(WP, W)]))):
        cp = pltpu.make_async_copy(src, dst, w_sem.at[i])
        cp.start()
        loads.append(cp)

    bar = pltpu.get_barrier_semaphore()
    peers = [partner, across] + [dev(s, z, ynb[i], c) for i in (1, 2, 3)]
    peers += [dev(ss, zz, y, c) for ss in (s_up, s_dn) for zz in (z, zo)]
    for peer in peers:
        pl.semaphore_signal(bar, inc=1, device_id=peer, device_id_type=MESH)

    sends = []

    def put(src, dst, ssem, rsem, to, keep=True):
        cp = pltpu.make_async_remote_copy(
            src_ref=src, dst_ref=dst, send_sem=ssem, recv_sem=rsem, device_id=to, device_id_type=MESH
        )
        cp.start()
        if keep:
            sends.append(cp)
        return cp

    def got(dst, ssem, rsem):
        pltpu.make_async_remote_copy(
            src_ref=dst, dst_ref=dst, send_sem=ssem, recv_sem=rsem, device_id=partner, device_id_type=MESH
        ).wait_recv()

    def sent(src, ssem, rsem):
        pltpu.make_async_remote_copy(
            src_ref=src, dst_ref=src, send_sem=ssem, recv_sem=rsem, device_id=partner, device_id_type=MESH
        ).wait_send()

    def pair(a, b):
        return jnp.concatenate([a.astype(F32), b.astype(F32)], axis=0).astype(BF16)

    gain = gain_ref[...].astype(F32)

    CA[0] = pair(c_act[0], c_act_t[0])
    CA[1] = pair(c_adj[0], c_adj_t[0])
    for k in range(2):
        ST[k, z] = pair(stash[0, k], stash_t[0, k])

    pl.semaphore_wait(bar, 9)

    @pl.when(s != 0)
    def _():
        for i in range(2):
            put(CA.at[1], G.at[A1, own[0]], ad_s.at[0, i], ad_r.at[0, z], dev(s_dn, zhs[i], y, c), keep=False)

    put(ST.at[0, z], ST.at[0, z], st_s.at[0], st_r.at[0], across)

    @pl.when(s != 15)
    def _():
        for i in range(2):
            put(CA.at[0], IN.at[0, z], in_s.at[0, i], in_r.at[0, z], dev(s_up, zhs[i], y, c), keep=False)

    zero = jnp.zeros((8, D), F32)

    @pl.when(s == 0)
    def _():
        for k in range(2):
            IN[k, z] = pair(fresh[k], zero)
            put(IN.at[k, z], IN.at[k, z], in_s.at[k, 2], in_r.at[k, z], across, keep=False)

    @pl.when(s == 15)
    def _():
        for k, g in enumerate((A1, A2)):
            G[g, own[0]] = pair(loss[k], zero)
            put(G.at[g, own[0]], G.at[g, own[0]], ad_s.at[k, 2], ad_r.at[k, z], across, keep=False)

    put(ST.at[1, z], ST.at[1, z], st_s.at[1], st_r.at[1], across)

    def wait_in(k, i):
        def go():
            got(IN.at[k, zhs[i]], in_s.at[k, 0], in_r.at[k, zhs[i]])

        if i == 0:
            pl.when(s != 0)(go)
        else:
            go()

    def wait_ad(k, i):
        def go():
            got(G.at[(A1, A2)[k], own[i]], ad_s.at[k, 0], ad_r.at[k, zhs[i]])

        if i == 0:
            pl.when(s != 15)(go)
        else:
            go()

    def send_own(g, i):
        ref = G.at[g, own[i]]
        for dd in (1, 3, 2):
            put(ref, ref, lane_s.at[g, dd - 1, i], lane_r.at[g, dd - 1, zhs[i]], dev(s, z, ynb[dd], c))
        put(ref, ref, part_s.at[g, 0, i], part_r.at[g, 0, zhs[i]], partner)

    def forward(g, i):
        for dd in (1, 3, 2):
            ref = G.at[g, slot(c, ysrc[dd], zhs[i])]
            got(ref, lane_s.at[g, dd - 1, i], lane_r.at[g, dd - 1, zhs[i]])
            put(ref, ref, part_s.at[g, dd, i], part_r.at[g, dd, zhs[i]], partner)

    def finish(g):
        for i in range(2):
            for dd in range(4):
                got(G.at[g, slot(co, ysrc[dd], zhs[i])], part_s.at[g, dd, i], part_r.at[g, dd, zhs[i]])

    def norm_to(g, ref, i):
        G[g, own[i]] = norm_pair(ref[zhs[i]].astype(F32), gain)

    def wide(g, weights):
        x = G[g].reshape(256, D)
        for j in range(3):
            AB[:, j * 256 : (j + 1) * 256] = lax.dot_general(
                x, weights[j * 256 : (j + 1) * 256, :], (((1,), (1,)), ((), ())), preferred_element_type=F32
            )
        r = AB[...].reshape(16, 16, 2 * WP)
        return r[:, :8, :WP], r[:, 8:, :WP] + r[:, :8, WP:]

    def left(X, v, vt):
        top = jnp.concatenate([v, jnp.zeros_like(v)], axis=2)
        low = jnp.concatenate([vt, v], axis=2)
        X[...] = jnp.concatenate([top, low], axis=1).reshape(256, 2 * WP).astype(BF16)

    def turned(v, vt):
        return jnp.concatenate([vt, v], axis=1).reshape(256, WP).astype(BF16)

    def rs_a(k, X, weights):
        for j in range(NC):
            wj = weights[:, j * CW : (j + 1) * CW]
            there = jnp.dot(X[pl.ds(pl.multiple_of(128 * co, 128), 128), :], wj, preferred_element_type=F32)
            PS[k, j] = there.astype(BF16)
            put(PS.at[k, j], PR.at[k, j], pr_s.at[k, j], pr_r.at[k, j], partner)
            OWN[k % 2, j] = jnp.dot(
                X[pl.ds(pl.multiple_of(128 * c, 128), 128), :], wj, preferred_element_type=F32
            )

    def rs_b(k):
        for j in range(NC):
            got(PR.at[k, j], pr_s.at[k, j], pr_r.at[k, j])
            total = OWN[k % 2, j] + PR[k, j].astype(F32)
            OWN[k % 2, j] = total
            YS[k, j] = total.astype(BF16).reshape(4, 32, CW)
            for dd in (2, 1, 3):
                put(YS.at[k, j, ynb[dd]], YR.at[k, j, dd - 1], yr_s.at[k, j, dd - 1], yr_r.at[k, j, dd - 1],
                    dev(s, z, ynb[dd], c))

    def rs_c(k):
        for j in range(NC):
            total = OWN[k % 2, j, pl.ds(pl.multiple_of(32 * y, 32), 32), :]
            for dd in (1, 3, 2):
                got(YR.at[k, j, dd - 1], yr_s.at[k, j, dd - 1], yr_r.at[k, j, dd - 1])
                total = total + YR[k, j, dd - 1].astype(F32)
            ZS[k, j] = total.astype(BF16).reshape(2, 16, CW)
            if k < 2:
                put(ZS.at[k, j], ZR.at[k, j], zr_s.at[k, j], zr_r.at[k, j], across)
            else:
                put(ZS.at[k, j, zo], ZR.at[k, j, zo], zr_s.at[k, j], zr_r.at[k, j], across)

    def rs_d(k):
        for j in range(NC):
            cols = slice(j * CW, (j + 1) * CW)
            if k < 2:
                got(ZR.at[k, j], zr_s.at[k, j], zr_r.at[k, j])
                FB[k % 2, :, :, cols] = ZS[k, j].astype(F32) + ZR[k, j].astype(F32)
            else:
                got(ZR.at[k, j, z], zr_s.at[k, j], zr_r.at[k, j])
                FB[k % 2, 0, :, cols] = ZS[k, j, z].astype(F32) + ZR[k, j, z].astype(F32)

    def forward_branch(tick):
        g, k = (N1, N2)[tick], (P1, P2)[tick]
        finish(g)
        a, at = wide(g, WU)
        g0, g1, _ = gelu_parts(a)
        left(XP, g0, g1 * at)
        rs_a(k, XP, WV)

    def backward_first(tick):
        g = (M1, M2)[tick]
        finish(g)
        return wide(g, WU)

    def backward_second(tick, b, bt):
        g, k = (A1, A2)[tick], (T1, T2)[tick]
        finish(g)
        g0, g1, g2 = gelu_parts(b)
        e, et = wide(g, WV)
        zv, zt = e * g1, et * g1 + e * g2 * bt
        left(XT, zv, zt)
        rs_a(k, XT, WU)
        QC[...] = turned(g0, g1 * bt)
        ZC[...] = turned(zv, zt)

    def curvature(tick):
        for lhs, acc, g, o in ((QC, CD, (A1, A2)[tick], 1), (ZC, CU, (M1, M2)[tick], 0)):
            lt = lhs[...].T[:W]
            x = G[g].reshape(256, D)
            for j in range(NC):
                cols = slice(j * CW, (j + 1) * CW)
                part = jnp.dot(lt, x[:, cols], preferred_element_type=F32)
                if tick == 0:
                    acc[:, cols] = part
                else:
                    CO[o, :, cols] = (acc[:, cols] + part).astype(BF16)

    norm_to(M1, ST.at[0], 0)
    send_own(M1, 0)
    wait_ad(0, 0)
    send_own(A1, 0)
    got(ST.at[0, zo], st_s.at[0], st_r.at[0])
    norm_to(M1, ST.at[0], 1)
    send_own(M1, 1)
    wait_ad(0, 1)
    send_own(A1, 1)
    forward(M1, 0)
    wait_in(0, 0)
    norm_to(N1, IN.at[0], 0)
    send_own(N1, 0)
    forward(A1, 0)
    wait_in(0, 1)
    norm_to(N1, IN.at[0], 1)
    send_own(N1, 1)
    for r in range(2):
        WU[r * WP + W : (r + 1) * WP, :] = jnp.zeros((WP - W, D), BF16)
        WV[r * WP + W : (r + 1) * WP, :] = jnp.zeros((WP - W, D), BF16)
    norm_to(M2, ST.at[1], 0)
    for cp in loads:
        cp.wait()
    forward(M1, 1)
    b, bt = backward_first(0)
    forward(A1, 1)
    backward_second(0, b, bt)
    forward(N1, 0)
    rs_b(T1)
    forward(N1, 1)
    forward_branch(0)
    rs_b(P1)
    got(ST.at[1, zo], st_s.at[1], st_r.at[1])
    norm_to(M2, ST.at[1], 1)
    send_own(M2, 0)
    send_own(M2, 1)
    rs_c(T1)
    curvature(0)

    rs_d(T1)
    for i in range(2):
        out, out_t = norm_back(ST[0, zhs[i]].astype(F32), G[A1, own[i]].astype(F32), FB[0, zhs[i]], gain)
        SH[0, zhs[i]] = jnp.concatenate([out, out_t], axis=0).astype(BF16)

    @pl.when(s != 0)
    def _():
        for i in range(2):
            put(SH.at[0, zhs[i]], G.at[A2, own[i]], ad_s.at[1, i], ad_r.at[1, zhs[i]], dev(s_dn, z, y, c), keep=False)

    rs_c(P1)
    rs_d(P1)
    SH[1] = (IN[0].astype(F32) + FB[1]).astype(BF16)

    @pl.when(s != 15)
    def _():
        for i in range(2):
            put(SH.at[1, zhs[i]], IN.at[1, zhs[i]], in_s.at[1, i], in_r.at[1, zhs[i]], dev(s_up, z, y, c), keep=False)

    forward(M2, 0)
    forward(M2, 1)
    for i in range(2):
        wait_ad(1, i)
        send_own(A2, i)
    for i in range(2):
        wait_in(1, i)
        norm_to(N2, IN.at[1], i)
        send_own(N2, i)
    b, bt = backward_first(1)
    forward(A2, 0)
    forward(A2, 1)
    backward_second(1, b, bt)
    forward(N2, 0)
    rs_b(T2)
    forward(N2, 1)
    forward_branch(1)
    rs_b(P2)
    curvature(1)
    outs = []
    for i, ref in enumerate((o_up, o_down)):
        cp = pltpu.make_async_copy(CO.at[i], ref, o_sem.at[i])
        cp.start()
        outs.append(cp)
    rs_c(T2)
    rs_c(P2)
    rs_d(T2)
    out, out_t = norm_back(ST[1, z].astype(F32), G[A2, own[0]].astype(F32), FB[0, 0], gain)
    o_adj[0] = out.astype(BF16)
    o_adj_t[0] = out_t.astype(BF16)
    rs_d(P2)
    result = IN[1, z].astype(F32) + FB[1, 0]
    o_act[0] = result[:8].astype(BF16)
    o_act_t[0] = result[8:].astype(BF16)

    for cp in outs:
        cp.wait()
    for cp in sends:
        cp.wait_send()

    @pl.when(s != 0)
    def _():
        for i in range(2):
            sent(CA.at[1], ad_s.at[0, i], ad_r.at[0, z])
            sent(SH.at[0, zhs[i]], ad_s.at[1, i], ad_r.at[1, z])

    @pl.when(s != 15)
    def _():
        for i in range(2):
            sent(CA.at[0], in_s.at[0, i], in_r.at[0, z])
            sent(SH.at[1, zhs[i]], in_s.at[1, i], in_r.at[1, z])

    @pl.when(s == 0)
    def _():
        for k in range(2):
            sent(IN.at[k, z], in_s.at[k, 2], in_r.at[k, z])

    @pl.when(s == 15)
    def _():
        for k, g in enumerate((A1, A2)):
            sent(G.at[g, own[0]], ad_s.at[k, 2], ad_r.at[k, z])


def shards(
    carry_act, carry_act_tan, carry_adj, carry_adj_tan, fresh_act, loss_cot, stash_act, stash_act_tan,
    norm_gain, up_weight, down_weight, up_dir, down_dir,
):
    rows = jax.ShapeDtypeStruct((1, 8, D), BF16)
    flat = jax.ShapeDtypeStruct((W, D), BF16)
    vmem, hbm = pl.BlockSpec(memory_space=pltpu.VMEM), pl.BlockSpec(memory_space=pl.ANY)
    dma = pltpu.SemaphoreType.DMA
    outs = pl.pallas_call(
        kernel,
        name="relay",
        out_shape=(rows, rows, rows, rows, flat, flat),
        in_specs=[vmem] * 9 + [hbm] * 4,
        out_specs=(vmem, vmem, vmem, vmem, hbm, hbm),
        scratch_shapes=[
            pltpu.VMEM((6, 16, 16, D), BF16),
            pltpu.VMEM((2, 2, 16, D), BF16),
            pltpu.VMEM((2, 2, 16, D), BF16),
            pltpu.VMEM((2, 16, D), BF16),
            pltpu.VMEM((2, 2, 16, D), BF16),
            pltpu.VMEM((2 * WP, D), BF16),
            pltpu.VMEM((2 * WP, D), BF16),
            pltpu.VMEM((256, 2 * WP), F32),
            pltpu.VMEM((256, 2 * WP), BF16),
            pltpu.VMEM((256, 2 * WP), BF16),
            pltpu.VMEM((256, WP), BF16),
            pltpu.VMEM((256, WP), BF16),
            pltpu.VMEM((2, NC, 128, CW), F32),
            pltpu.VMEM((4, NC, 128, CW), BF16),
            pltpu.VMEM((4, NC, 128, CW), BF16),
            pltpu.VMEM((4, NC, 4, 32, CW), BF16),
            pltpu.VMEM((4, NC, 3, 32, CW), BF16),
            pltpu.VMEM((4, NC, 2, 16, CW), BF16),
            pltpu.VMEM((4, NC, 2, 16, CW), BF16),
            pltpu.VMEM((2, 2, 16, D), F32),
            pltpu.VMEM((W, D), F32),
            pltpu.VMEM((W, D), F32),
            pltpu.VMEM((2, W, D), BF16),
            dma((4,)),
            dma((2,)),
            dma((6, 3, 2)),
            dma((6, 3, 2)),
            dma((6, 4, 2)),
            dma((6, 4, 2)),
            dma((4, NC)),
            dma((4, NC)),
            dma((4, NC, 3)),
            dma((4, NC, 3)),
            dma((4, NC)),
            dma((4, NC)),
            dma((2, 2)),
            dma((2, 3)),
            dma((2, 2)),
            dma((2, 3)),
            dma((2,)),
            dma((2,)),
        ],
        compiler_params=pltpu.CompilerParams(
            collective_id=0, has_side_effects=True, vmem_limit_bytes=60 * 1024 * 1024
        ),
    )(
        carry_act, carry_act_tan, carry_adj, carry_adj_tan, fresh_act, loss_cot, stash_act, stash_act_tan, norm_gain,
        up_weight[0].T, down_weight[0], up_dir[0].T, down_dir[0],
    )
    return outs[0], outs[1], outs[2], outs[3], outs[4].T[None], outs[5][None]


def solution(mesh):
    rows = P("section", "dp", None)
    in_specs = (
        rows, rows, rows, rows,
        P(None, "dp", None), P(None, "dp", None),
        P("section", None, "dp", None), P("section", None, "dp", None),
        P("section", None),
        P("section", None, "dp"), rows, P("section", None, "dp"), rows,
    )
    out_specs = (rows, rows, rows, rows, P("section", None, "dp"), rows)
    return jax.shard_map(shards, mesh=mesh, in_specs=in_specs, out_specs=out_specs, check_vma=False)
```

time: 453 us -> 114 us (0.25)
  waiting for transfers between devices: 297 us -> 0 us
  Pallas kernels: 0 us -> 103 us
  matrix products: 60.4 us -> 0 us
  starting transfers between devices: 30.6 us -> 0 us
  other arithmetic: 20.1 us -> 0 us
  local copies, waits for them, and re-layouts: 25.1 us -> 9.18 us
  between operations: 14.7 us -> 0.65 us
    reduce_scatter x2 -> x0, waiting for transfers between devices: 157 us -> none  [one_scatter(): lax.psum_scatter(lines, axis, tiled=True).reshape(-1)]
    all_gather x2 -> x0, waiting for transfers between devices: 141 us -> none  [in_one_piece(): whole, at, done = (lax.all_gather(both, axis, axis=dim, tiled=True), 0, [])]
    pallas_call x0 -> x1, Pallas kernels: none -> 103 us  [shards(): pl.pallas_call(kernel, name='relay', out_shape=(rows, rows, rows, rows, f...]
    dot_general x36 -> x0, matrix products: 60.4 us -> none  [the longest x16 33.7 us: matrix_product(): return jnp.dot(left, right, preferred_element_type=jnp.float32)]
    ppermute x8 -> x0, starting transfers between devices: 30.2 us -> none  [passed_along(): lax.ppermute(value, axis, [(source, source + steps) for source in range(l...]
    another operation x8 -> x0, local copies, waits for them, and re-layouts: 13.9 us -> none  [one_scatter(): lines = jnp.concatenate([b.reshape(length, -1) for b in parts], axis=1)]
    reshape x2 -> x0, local copies, waits for them, and re-layouts: 6.88 us -> none  [one_scatter(): jnp.pad(lines, ((0, 0), (0, rows * 128 - lines.shape[1]))).reshape(-1, 128)]
    concatenate x4 -> x0, other arithmetic: 5.62 us -> none  [the longest x2 5.59 us: one_scatter(): lines = jnp.concatenate([b.reshape(length, -1) for b in parts], axis=1)]
  transfers between devices with their start and end apart: 12 -> 0, of which waited for: 4 -> 0; matrix products, arithmetic and copies ran while one was open for 4% -> 0% of each run, Pallas kernels for 0% -> 0%
where the time goes in v1:
time: 114 us; the launch traced here: 113 us
  Pallas kernels  103 us (90%)
  local copies, waits for them, and re-layouts  9.18 us (8%)
    pallas_call x1, Pallas kernels, shards(): pl.pallas_call(kernel, name='relay', out_shape=(rows, rows, rows, rows, f...  103 us
    unnamed x8, local copies, waits for them, and re-layouts  9.18 us

profile of v1, /device:TPU:32, one launch (start us, length us, event | category | flops | bytes accessed | tf_op | source)
XLA Modules:
  0.0 113.1 jit_solution(3945276736947582944)
XLA Ops:
  0.6 103.3 %relay.1 = (bf16[1,8,2304]{2,1,0:T(8,128)(2,1)}, bf16[1,8,2304]{2,1,0:T(8,128)(2,1)}, bf16[1,8,2304]{2,1,0:T(8,128)(2,1)}, bf16[1,8,2304]{2,1,0:T(8,128)(2,1)}, ...) custom-call(bf16[1,8,2304]{2,1,0:T(8,128)(2,1)} %c_act.1, bf16[1,8,2304]{2,1,0:T(8,128)(2,1)} %c_act_t.1, ...), custom_call_target="tpu_custom_call" | custom-call | tf_op jit(solution)/shard_map/relay/pallas_call | solution.py:427
  104.0 1.4 %copy.25 = bf16[1,8,2304]{2,1,0:T(8,128)(2,1)} copy(bf16[1,8,2304]{2,1,0:T(8,128)(2,1)} %get-tuple-element.24) | data formatting | bytes 73728
  105.3 1.4 %copy.26 = bf16[1,8,2304]{2,1,0:T(8,128)(2,1)} copy(bf16[1,8,2304]{2,1,0:T(8,128)(2,1)} %get-tuple-element.25) | data formatting | bytes 73728
  106.7 1.4 %copy.27 = bf16[1,8,2304]{2,1,0:T(8,128)(2,1)} copy(bf16[1,8,2304]{2,1,0:T(8,128)(2,1)} %get-tuple-element.26) | data formatting | bytes 73728
  108.1 1.4 %copy.28 = bf16[1,8,2304]{2,1,0:T(8,128)(2,1)} copy(bf16[1,8,2304]{2,1,0:T(8,128)(2,1)} %get-tuple-element.27) | data formatting | bytes 73728
  109.5 0.0 copy-start
  109.5 2.6 %copy.29 = bf16[1,2304,288]{1,2,0:T(8,128)(2,1)} copy(bf16[1,2304,288]{1,2,0:T(8,128)(2,1)} %bitcast.13) | data formatting | bytes 2654208
  112.1 0.0 copy-done
  112.1 1.1 copy.30
Async XLA Ops:
  109.5 2.6 %copy-start = (bf16[288,2304]{1,0:T(8,128)(2,1)S(1)}, bf16[288,2304]{1,0:T(8,128)(2,1)}, u32[]{:S(2)}) copy-start(bf16[288,2304]{1,0:T(8,128)(2,1)} %get-tuple-element.17) | copy-start | bytes 3981316

commit v2 on v1

v2 whole, which is shorter than its diff:
```python
import jax
import jax.numpy as jnp
from jax import lax
from jax.experimental import pallas as pl
from jax.experimental.pallas import tpu as pltpu
from jax.sharding import PartitionSpec as P

MESH = pl.DeviceIdType.MESH
F32, BF16 = jnp.float32, jnp.bfloat16

ROOT = 0.7978845608028654
CUBIC = 0.044715
EPS = 1e-06

D = 2304
W = 288
WP = 384
NC = 3
CW = D // NC
M1, A1, N1, M2, A2, N2 = range(6)
RING = {M1: (1, 0), A1: (3, 0), N1: (1, 0), M2: (3, 0), A2: (0, 0), N2: (0, 0)}
T1, P1, T2, P2 = range(4)


def gelu_parts(v):
    u = ROOT * (v + CUBIC * v * v * v)
    s1 = ROOT * (1.0 + 3.0 * CUBIC * v * v)
    s2 = 6.0 * ROOT * CUBIC * v
    th = jnp.tanh(u)
    sech = 1.0 - th * th
    g0 = 0.5 * v * (1.0 + th)
    g1 = 0.5 * (1.0 + th) + 0.5 * v * sech * s1
    g2 = sech * (s1 - v * th * s1 * s1 + 0.5 * v * s2)
    return g0, g1, g2


def stats(r, rt):
    inv = lax.rsqrt(jnp.mean(r * r, axis=-1, keepdims=True) + EPS)
    inv_t = -(inv * inv * inv) * jnp.mean(r * rt, axis=-1, keepdims=True)
    return inv, inv_t


def norm_pair(block, gain):
    r, rt = block[:8], block[8:]
    inv, inv_t = stats(r, rt)
    return jnp.concatenate([r * inv * gain, (rt * inv + r * inv_t) * gain], axis=0).astype(BF16)


def norm_back(block, arriving, grads, gain):
    x, xt = block[:8], block[8:]
    inv, inv_t = stats(x, xt)
    w, wt = grads[:8] * gain, grads[8:] * gain
    mu = jnp.mean(x * w, axis=-1, keepdims=True)
    mu_t = jnp.mean(xt * w + x * wt, axis=-1, keepdims=True)
    cube = inv * inv * inv
    out = arriving[:8] + inv * w - cube * x * mu
    out_t = (
        arriving[8:]
        + inv_t * w
        + inv * wt
        - 3.0 * inv * inv * inv_t * x * mu
        - cube * xt * mu
        - cube * x * mu_t
    )
    return out, out_t


def kernel(*refs):
    up_h, down_h, upd_h, downd_h = refs[9:13]
    o_act, o_act_t, o_adj, o_adj_t, o_up, o_down = refs[13:19]
    small = c_act, c_act_t, c_adj, c_adj_t, fresh, loss, stash, stash_t, gain_ref = refs[19:28]
    G, ST, IN, CA, SH, WU, WV, WUT, WVT, AB, GL, XT, XP, QC, ZC, OWN, PS, PR, YS, YR, ZS, ZR, FB, CU, CD = refs[28:53]
    (i_sem, w_sem, lane_r, lane_s, part_r, part_s, pr_r, pr_s, yr_r, yr_s, zr_r, zr_s,
     in_r, in_s, ad_r, ad_s, st_r, st_s) = refs[53:]
    s, d = lax.axis_index("section"), lax.axis_index("dp")
    z, y, c = lax.div(d, 8), lax.rem(lax.div(d, 2), 4), lax.rem(d, 2)
    zo, co = 1 - z, 1 - c
    s_up, s_dn = lax.rem(s + 1, 16), lax.rem(s + 15, 16)

    def dev(ss, zz, yy, cc):
        return (ss, zz * 8 + yy * 2 + cc)

    def slot(cc, yy, zz):
        return cc * 8 + yy * 2 + zz

    ynb = [y, lax.rem(y + 1, 4), lax.rem(y + 2, 4), lax.rem(y + 3, 4)]
    ysrc = [y, ynb[3], ynb[2], ynb[1]]
    partner = dev(s, z, y, co)
    across = dev(s, zo, y, c)
    own = [slot(c, y, z), slot(c, y, zo)]
    zhs = [z, zo]

    firsts = [pltpu.make_async_copy(a, b, i_sem.at[i]) for i, (a, b) in enumerate(zip(refs[:9], small))]
    for i in (6, 7, 2, 3, 0, 1, 8, 4, 5):
        firsts[i].start()

    loads = []
    for i, (src, dst) in enumerate(((up_h, WU.at[pl.ds(0, W)]), (upd_h, WU.at[pl.ds(WP, W)]),
                                    (down_h, WV.at[pl.ds(0, W)]), (downd_h, WV.at[pl.ds(WP, W)]))):
        cp = pltpu.make_async_copy(src, dst, w_sem.at[i])
        cp.start()
        loads.append(cp)

    bar = pltpu.get_barrier_semaphore()
    peers = [partner, across] + [dev(s, z, ynb[i], c) for i in (1, 2, 3)]
    peers += [dev(ss, zz, y, c) for ss in (s_up, s_dn) for zz in (z, zo)]
    for peer in peers:
        pl.semaphore_signal(bar, inc=1, device_id=peer, device_id_type=MESH)

    sends = []

    def put(src, dst, ssem, rsem, to, keep=True):
        cp = pltpu.make_async_remote_copy(
            src_ref=src, dst_ref=dst, send_sem=ssem, recv_sem=rsem, device_id=to, device_id_type=MESH
        )
        cp.start()
        if keep:
            sends.append(cp)
        return cp

    def got(dst, ssem, rsem):
        pltpu.make_async_remote_copy(
            src_ref=dst, dst_ref=dst, send_sem=ssem, recv_sem=rsem, device_id=partner, device_id_type=MESH
        ).wait_recv()

    def sent(src, ssem, rsem):
        pltpu.make_async_remote_copy(
            src_ref=src, dst_ref=src, send_sem=ssem, recv_sem=rsem, device_id=partner, device_id_type=MESH
        ).wait_send()

    def pair(a, b):
        return jnp.concatenate([a.astype(F32), b.astype(F32)], axis=0).astype(BF16)

    for cp in firsts:
        cp.wait()
    gain = gain_ref[...].astype(F32)

    CA[0] = pair(c_act[0], c_act_t[0])
    CA[1] = pair(c_adj[0], c_adj_t[0])
    for k in range(2):
        ST[k, z] = pair(stash[0, k], stash_t[0, k])

    pl.semaphore_wait(bar, 9)

    for i in range(2):

        @pl.when(s != 0)
        def _():
            put(CA.at[1], G.at[A1, own[0]], ad_s.at[0, i], ad_r.at[0, z], dev(s_dn, zhs[i], y, c), keep=False)

        if i == 1:
            continue

        @pl.when(s != 15)
        def _():
            put(CA.at[0], IN.at[0, z], in_s.at[0, i], in_r.at[0, z], dev(s_up, zhs[i], y, c), keep=False)

        put(ST.at[0, z], ST.at[0, z], st_s.at[0], st_r.at[0], across)

    @pl.when(s != 15)
    def _():
        put(CA.at[0], IN.at[0, z], in_s.at[0, 1], in_r.at[0, z], dev(s_up, zo, y, c), keep=False)

    zero = jnp.zeros((8, D), F32)

    @pl.when(s == 0)
    def _():
        for k in range(2):
            IN[k, z] = pair(fresh[k], zero)
            put(IN.at[k, z], IN.at[k, z], in_s.at[k, 2], in_r.at[k, z], across, keep=False)

    @pl.when(s == 15)
    def _():
        for k, g in enumerate((A1, A2)):
            G[g, own[0]] = pair(loss[k], zero)
            put(G.at[g, own[0]], G.at[g, own[0]], ad_s.at[k, 2], ad_r.at[k, z], across, keep=False)

    put(ST.at[1, z], ST.at[1, z], st_s.at[1], st_r.at[1], across)

    def wait_in(k, i, zz):
        def go():
            got(IN.at[k, zz], in_s.at[k, 0], in_r.at[k, zz])

        if k == 0 and i == 1:
            go()
        else:
            pl.when((s != 0) | (z != zz))(go)

    def wait_ad(k, i, zz):
        def go():
            ref = G.at[(A1, A2)[k], slot(c, y, zz)]
            got(ref, ad_s.at[k, 0], ad_r.at[k, zz])

        if k == 0 and i == 1:
            go()
        else:
            pl.when((s != 15) | (z != zz))(go)

    def send_own(g, i, zz):
        ref = G.at[g, slot(c, y, zz)]
        for dd in (1, 3) if RING[g][i] else (2, 1, 3):
            put(ref, ref, lane_s.at[g, dd - 1, i], lane_r.at[g, dd - 1, i], dev(s, z, ynb[dd], c))
        put(ref, ref, part_s.at[g, 0, i], part_r.at[g, 0, i], partner)

    def pass_on(g, i, zz, dds):
        for dd in dds:
            ref = G.at[g, slot(c, ysrc[dd], zz)]
            got(ref, lane_s.at[g, dd - 1, i], lane_r.at[g, dd - 1, i])
            if RING[g][i] == dd:
                put(ref, ref, lane_s.at[g, 1, i], lane_r.at[g, 1, i], dev(s, z, ynb[dd], c))
            put(ref, ref, part_s.at[g, dd, i], part_r.at[g, dd, i], partner)

    def near(g, i, zz):
        pass_on(g, i, zz, (1, 3))

    def far(g, i, zz):
        pass_on(g, i, zz, (2,))

    def both(g, i, zz):
        pass_on(g, i, zz, (1, 3, 2))

    def finish(g, order):
        for i in range(2):
            for dd in range(4):
                got(G.at[g, slot(co, ysrc[dd], order[i])], part_s.at[g, dd, i], part_r.at[g, dd, i])

    def norm_to(g, ref, zz):
        G[g, slot(c, y, zz)] = norm_pair(ref[zz].astype(F32), gain)

    def turn(weights, turned_weights):
        for j in range(9):
            cols = slice(j * 256, (j + 1) * 256)
            turned_weights[cols, :] = weights[:, cols].T

    def wide(n, g, weights, cc):
        x = G[g, pl.ds(8 * cc, 8)].reshape(128, D)
        for j in range(3):
            cols = slice(j * 256, (j + 1) * 256)
            AB[n, pl.ds(pl.multiple_of(128 * cc, 128), 128), cols] = jnp.dot(
                x, weights[:, cols], preferred_element_type=F32
            )

    def widened(n):
        r = AB[n].reshape(16, 16, 2 * WP)
        return r[:, :8, :WP], r[:, 8:, :WP] + r[:, :8, WP:]

    def left(X, v, vt):
        top = jnp.concatenate([v, jnp.zeros_like(v)], axis=2)
        low = jnp.concatenate([vt, v], axis=2)
        X[...] = jnp.concatenate([top, low], axis=1).reshape(256, 2 * WP).astype(BF16)

    def turned(v, vt):
        return jnp.concatenate([vt, v], axis=1).reshape(256, WP).astype(BF16)

    def reduce_a(k, X, weights):
        for j in range(NC):
            wj = weights[:, j * CW : (j + 1) * CW]
            there = jnp.dot(X[pl.ds(pl.multiple_of(128 * co, 128), 128), :], wj, preferred_element_type=F32)
            PS[k, j] = there.astype(BF16)
            put(PS.at[k, j], PR.at[k, j], pr_s.at[k, j], pr_r.at[k, j], partner)

    def reduce_b(k, X, weights, zz):
        for j in range(NC):
            wj = weights[:, j * CW : (j + 1) * CW]
            here = jnp.dot(X[pl.ds(pl.multiple_of(128 * c, 128), 128), :], wj, preferred_element_type=F32)
            got(PR.at[k, j], pr_s.at[k, j], pr_r.at[k, j])
            total = here + PR[k, j].astype(F32)
            OWN[k % 2, j] = total
            YS[k, :, :, j] = total.astype(BF16).reshape(4, 2, 16, CW)
            reduce_y(k, 0, zz, j)

    def reduce_y(k, i, zz, j):
        for dd in (2, 1, 3):
            put(YS.at[k, ynb[dd], zz, j], YR.at[k, zz, dd - 1, j], yr_s.at[k, i, dd - 1, j], yr_r.at[k, i, dd - 1, j],
                dev(s, z, ynb[dd], c))

    def reduce_more(k, zz):
        for j in range(NC):
            reduce_y(k, 1, zz, j)

    def reduce_z(k, i, zz):
        for j in range(NC):
            for dd in (1, 3, 2):
                got(YR.at[k, zz, dd - 1, j], yr_s.at[k, i, dd - 1, j], yr_r.at[k, i, dd - 1, j])
            total = OWN[k % 2, j, pl.ds(pl.multiple_of(32 * y + 16 * zz, 16), 16), :]
            for dd in (1, 3, 2):
                total = total + YR[k, zz, dd - 1, j].astype(F32)
            if k < 2 or i == 0:
                ZS[k, zz, j] = total.astype(BF16)
                put(ZS.at[k, zz, j], ZR.at[k, zz, j], zr_s.at[k, i, j], zr_r.at[k, i, j], across)
            else:
                FB[k % 2, zz, :, j * CW : (j + 1) * CW] = total

    def reduce_end(k, i, zz):
        for j in range(NC):
            got(ZR.at[k, zz, j], zr_s.at[k, i, j], zr_r.at[k, i, j])
            cols = slice(j * CW, (j + 1) * CW)
            mine = ZS[k, zz, j].astype(F32) if k < 2 else FB[k % 2, zz, :, cols]
            FB[k % 2, zz, :, cols] = mine + ZR[k, zz, j].astype(F32)

    def forward_branch(tick):
        a, at = widened(0)
        g0, g1, _ = gelu_parts(a)
        left(XP, g0, g1 * at)
        reduce_a((P1, P2)[tick], XP, WV)

    def forward_rest(tick):
        reduce_b((P1, P2)[tick], XP, WV, (0, zo)[tick])

    def backward_first():
        b, bt = widened(1)
        g0, g1, g2 = gelu_parts(b)
        GL[0], GL[1] = g1, g2 * bt
        QC[...] = turned(g0, g1 * bt)

    def backward_second(tick):
        e, et = widened(2)
        zv, zt = e * GL[0], et * GL[0] + e * GL[1]
        left(XT, zv, zt)
        reduce_a((T1, T2)[tick], XT, WU)
        ZC[...] = turned(zv, zt)
        reduce_b((T1, T2)[tick], XT, WU, (0, zo)[tick])

    def curvature(tick, which):
        for lhs, acc, g, o in (((QC, CD, (A1, A2)[tick], 1), (ZC, CU, (M1, M2)[tick], 0))[which],):
            lt = lhs[...].T[:W]
            x = G[g].reshape(256, D)
            for j in range(NC):
                cols = slice(j * CW, (j + 1) * CW)
                part = jnp.dot(lt, x[:, cols], preferred_element_type=F32)
                if tick == 0:
                    acc[:, cols] = part
                else:
                    (o_up, o_down)[o][:, cols] = (acc[:, cols] + part).astype(BF16)

    def next_adjoint(zz):
        out, out_t = norm_back(ST[0, zz].astype(F32), G[A1, slot(c, y, zz)].astype(F32), FB[0, zz], gain)
        SH[0, zz] = jnp.concatenate([out, out_t], axis=0).astype(BF16)

        @pl.when(s != 0)
        def _():
            put(SH.at[0, zz], G.at[A2, slot(c, y, zz)], ad_s.at[1, zz], ad_r.at[1, zz], dev(s_dn, z, y, c), keep=False)

    def next_input(zz):
        SH[1, zz] = (IN[0, zz].astype(F32) + FB[1, zz]).astype(BF16)

        @pl.when(s != 15)
        def _():
            put(SH.at[1, zz], IN.at[1, zz], in_s.at[1, zz], in_r.at[1, zz], dev(s_up, z, y, c), keep=False)

    with jax.named_scope("p00_norm_to_M1_ST_at_0_z"):
        norm_to(M1, ST.at[0], z)
    with jax.named_scope("p01_send_own_M1_0_z"):
        send_own(M1, 0, z)
    with jax.named_scope("p02_norm_to_M2_ST_at_1_z"):
        norm_to(M2, ST.at[1], z)
    with jax.named_scope("p03_send_own_M2_0_z"):
        send_own(M2, 0, z)
    for r in range(2):
        WU[r * WP + W : (r + 1) * WP, :] = jnp.zeros((WP - W, D), BF16)
        WV[r * WP + W : (r + 1) * WP, :] = jnp.zeros((WP - W, D), BF16)
    with jax.named_scope("p04_wait_ad_0_0_z"):
        wait_ad(0, 0, z)
    with jax.named_scope("p05_send_own_A1_0_z"):
        send_own(A1, 0, z)
    with jax.named_scope("p06_near_M1_0_z"):
        near(M1, 0, z)
    for cp in loads:
        cp.wait()
    with jax.named_scope("p07_turn_WU_WUT"):
        turn(WU, WUT)
    with jax.named_scope("p08_got_ST_at_0_zo_st_s_at_0"):
        got(ST.at[0, zo], st_s.at[0], st_r.at[0])
    with jax.named_scope("p09_norm_to_M1_ST_at_0_zo"):
        norm_to(M1, ST.at[0], zo)
    with jax.named_scope("p10_send_own_M1_1_zo"):
        send_own(M1, 1, zo)
    with jax.named_scope("p11_near_A1_0_z"):
        near(A1, 0, z)
    with jax.named_scope("p12_near_M2_0_z"):
        near(M2, 0, z)
    with jax.named_scope("p13_turn_WV_WVT"):
        turn(WV, WVT)
    with jax.named_scope("p14_wait_in_0_0_z"):
        wait_in(0, 0, z)
    with jax.named_scope("p15_norm_to_N1_IN_at_0_z"):
        norm_to(N1, IN.at[0], z)
    with jax.named_scope("p16_wait_ad_0_1_zo"):
        wait_ad(0, 1, zo)
    with jax.named_scope("p17_send_own_A1_1_zo"):
        send_own(A1, 1, zo)
    with jax.named_scope("p18_send_own_N1_0_z"):
        send_own(N1, 0, z)
    with jax.named_scope("p19_far_M1_0_z"):
        far(M1, 0, z)
    with jax.named_scope("p20_both_M1_1_zo"):
        both(M1, 1, zo)
    with jax.named_scope("p21_wide_1_M1_WUT_c"):
        wide(1, M1, WUT, c)
    with jax.named_scope("p22_wait_in_0_1_zo"):
        wait_in(0, 1, zo)
    with jax.named_scope("p23_norm_to_N1_IN_at_0_zo"):
        norm_to(N1, IN.at[0], zo)
    with jax.named_scope("p24_send_own_N1_1_zo"):
        send_own(N1, 1, zo)
    with jax.named_scope("p25_finish_M1_z_zo"):
        finish(M1, (z, zo))
    with jax.named_scope("p26_wide_1_M1_WUT_co"):
        wide(1, M1, WUT, co)
    with jax.named_scope("p27_far_A1_0_z"):
        far(A1, 0, z)
    with jax.named_scope("p28_both_A1_1_zo"):
        both(A1, 1, zo)
    with jax.named_scope("p29_near_N1_0_z"):
        near(N1, 0, z)
    with jax.named_scope("p30_got_ST_at_1_zo_st_s_at_1"):
        got(ST.at[1, zo], st_s.at[1], st_r.at[1])
    with jax.named_scope("p31_norm_to_M2_ST_at_1_zo"):
        norm_to(M2, ST.at[1], zo)
    with jax.named_scope("p32_send_own_M2_1_zo"):
        send_own(M2, 1, zo)
    with jax.named_scope("p33_backward_first"):
        backward_first()
    with jax.named_scope("p34_wide_2_A1_WVT_c"):
        wide(2, A1, WVT, c)
    with jax.named_scope("p35_finish_A1_z_zo"):
        finish(A1, (z, zo))
    with jax.named_scope("p36_wide_2_A1_WVT_co"):
        wide(2, A1, WVT, co)
    with jax.named_scope("p37_backward_second_0"):
        backward_second(0)
    with jax.named_scope("p38_reduce_more_T1_1"):
        reduce_more(T1, 1)
    with jax.named_scope("p39_far_N1_0_z"):
        far(N1, 0, z)
    with jax.named_scope("p40_both_N1_1_zo"):
        both(N1, 1, zo)
    with jax.named_scope("p41_wide_0_N1_WUT_c"):
        wide(0, N1, WUT, c)
    with jax.named_scope("p42_finish_N1_z_zo"):
        finish(N1, (z, zo))
    with jax.named_scope("p43_wide_0_N1_WUT_co"):
        wide(0, N1, WUT, co)
    with jax.named_scope("p44_forward_branch_0"):
        forward_branch(0)
    with jax.named_scope("p45_reduce_z_T1_0_0"):
        reduce_z(T1, 0, 0)
    with jax.named_scope("p46_forward_rest_0"):
        forward_rest(0)
    with jax.named_scope("p47_reduce_more_P1_1"):
        reduce_more(P1, 1)
    with jax.named_scope("p48_far_M2_0_z"):
        far(M2, 0, z)
    with jax.named_scope("p49_both_M2_1_zo"):
        both(M2, 1, zo)
    with jax.named_scope("p50_reduce_z_T1_1_1"):
        reduce_z(T1, 1, 1)
    with jax.named_scope("p51_curvature_0_0"):
        curvature(0, 0)
    with jax.named_scope("p52_reduce_end_T1_0_0"):
        reduce_end(T1, 0, 0)
    with jax.named_scope("p53_next_adjoint_0"):
        next_adjoint(0)
    with jax.named_scope("p54_reduce_z_P1_0_0"):
        reduce_z(P1, 0, 0)
    with jax.named_scope("p55_curvature_0_1"):
        curvature(0, 1)
    with jax.named_scope("p56_reduce_end_T1_1_1"):
        reduce_end(T1, 1, 1)
    with jax.named_scope("p57_next_adjoint_1"):
        next_adjoint(1)
    with jax.named_scope("p58_reduce_z_P1_1_1"):
        reduce_z(P1, 1, 1)
    with jax.named_scope("p59_wait_ad_1_0_0"):
        wait_ad(1, 0, 0)
    with jax.named_scope("p60_send_own_A2_0_0"):
        send_own(A2, 0, 0)
    with jax.named_scope("p61_reduce_end_P1_0_0"):
        reduce_end(P1, 0, 0)
    with jax.named_scope("p62_next_input_0"):
        next_input(0)
    with jax.named_scope("p63_wait_ad_1_1_1"):
        wait_ad(1, 1, 1)
    with jax.named_scope("p64_send_own_A2_1_1"):
        send_own(A2, 1, 1)
    with jax.named_scope("p65_wide_1_M2_WUT_c"):
        wide(1, M2, WUT, c)
    with jax.named_scope("p66_finish_M2_z_zo"):
        finish(M2, (z, zo))
    with jax.named_scope("p67_wide_1_M2_WUT_co"):
        wide(1, M2, WUT, co)
    with jax.named_scope("p68_reduce_end_P1_1_1"):
        reduce_end(P1, 1, 1)
    with jax.named_scope("p69_next_input_1"):
        next_input(1)
    with jax.named_scope("p70_backward_first"):
        backward_first()
    with jax.named_scope("p71_both_A2_0_0"):
        both(A2, 0, 0)
    with jax.named_scope("p72_wait_in_1_0_0"):
        wait_in(1, 0, 0)
    with jax.named_scope("p73_norm_to_N2_IN_at_1_0"):
        norm_to(N2, IN.at[1], 0)
    with jax.named_scope("p74_send_own_N2_0_0"):
        send_own(N2, 0, 0)
    with jax.named_scope("p75_both_A2_1_1"):
        both(A2, 1, 1)
    with jax.named_scope("p76_wide_2_A2_WVT_c"):
        wide(2, A2, WVT, c)
    with jax.named_scope("p77_wait_in_1_1_1"):
        wait_in(1, 1, 1)
    with jax.named_scope("p78_norm_to_N2_IN_at_1_1"):
        norm_to(N2, IN.at[1], 1)
    with jax.named_scope("p79_send_own_N2_1_1"):
        send_own(N2, 1, 1)
    with jax.named_scope("p80_finish_A2_0_1"):
        finish(A2, (0, 1))
    with jax.named_scope("p81_wide_2_A2_WVT_co"):
        wide(2, A2, WVT, co)
    with jax.named_scope("p82_backward_second_1"):
        backward_second(1)
    with jax.named_scope("p83_reduce_more_T2_z"):
        reduce_more(T2, z)
    with jax.named_scope("p84_both_N2_0_0"):
        both(N2, 0, 0)
    with jax.named_scope("p85_both_N2_1_1"):
        both(N2, 1, 1)
    with jax.named_scope("p86_wide_0_N2_WUT_c"):
        wide(0, N2, WUT, c)
    with jax.named_scope("p87_finish_N2_0_1"):
        finish(N2, (0, 1))
    with jax.named_scope("p88_wide_0_N2_WUT_co"):
        wide(0, N2, WUT, co)
    with jax.named_scope("p89_forward_branch_1"):
        forward_branch(1)
    with jax.named_scope("p90_forward_rest_1"):
        forward_rest(1)
    with jax.named_scope("p91_reduce_more_P2_z"):
        reduce_more(P2, z)
    with jax.named_scope("p92_reduce_z_T2_0_zo"):
        reduce_z(T2, 0, zo)
    with jax.named_scope("p93_curvature_1_0"):
        curvature(1, 0)
    with jax.named_scope("p94_curvature_1_1"):
        curvature(1, 1)
    with jax.named_scope("p95_reduce_z_T2_1_z"):
        reduce_z(T2, 1, z)
    with jax.named_scope("p96_reduce_z_P2_0_zo"):
        reduce_z(P2, 0, zo)
    with jax.named_scope("p97_reduce_end_T2_0_z"):
        reduce_end(T2, 0, z)
    out, out_t = norm_back(ST[1, z].astype(F32), G[A2, own[0]].astype(F32), FB[0, z], gain)
    o_adj[0] = out.astype(BF16)
    o_adj_t[0] = out_t.astype(BF16)
    with jax.named_scope("p98_reduce_z_P2_1_z"):
        reduce_z(P2, 1, z)
    with jax.named_scope("p99_reduce_end_P2_0_z"):
        reduce_end(P2, 0, z)
    result = IN[1, z].astype(F32) + FB[1, z]
    o_act[0] = result[:8].astype(BF16)
    o_act_t[0] = result[8:].astype(BF16)

    for cp in sends:
        cp.wait_send()

    @pl.when(s != 0)
    def _():
        for i in range(2):
            sent(CA.at[1], ad_s.at[0, i], ad_r.at[0, z])
            sent(SH.at[0, i], ad_s.at[1, i], ad_r.at[1, z])

    @pl.when(s != 15)
    def _():
        for i in range(2):
            sent(CA.at[0], in_s.at[0, i], in_r.at[0, z])
            sent(SH.at[1, i], in_s.at[1, i], in_r.at[1, z])

    @pl.when(s == 0)
    def _():
        for k in range(2):
            sent(IN.at[k, z], in_s.at[k, 2], in_r.at[k, z])

    @pl.when(s == 15)
    def _():
        for k, g in enumerate((A1, A2)):
            sent(G.at[g, own[0]], ad_s.at[k, 2], ad_r.at[k, z])


def results(*refs):
    srcs, dsts, sem = refs[:6], refs[6:12], refs[12]
    copies = [pltpu.make_async_copy(a, b, sem.at[i]) for i, (a, b) in enumerate(zip(srcs, dsts))]
    for cp in copies:
        cp.start()
    for cp in copies:
        cp.wait()


def shards(
    carry_act, carry_act_tan, carry_adj, carry_adj_tan, fresh_act, loss_cot, stash_act, stash_act_tan,
    norm_gain, up_weight, down_weight, up_dir, down_dir,
):
    rows = jax.ShapeDtypeStruct((1, 8, D), BF16)
    flat = jax.ShapeDtypeStruct((W, D), BF16)
    vmem, hbm = pl.BlockSpec(memory_space=pltpu.VMEM), pl.BlockSpec(memory_space=pl.ANY)
    dma = pltpu.SemaphoreType.DMA
    small = (
        carry_act, carry_act_tan, carry_adj, carry_adj_tan, fresh_act, loss_cot, stash_act, stash_act_tan, norm_gain,
    )
    outs = pl.pallas_call(
        kernel,
        name="relay",
        out_shape=[pltpu.VMEM(a.shape, a.dtype) for a in (rows, rows, rows, rows, flat, flat)],
        in_specs=[pl.BlockSpec(memory_space=pltpu.HBM)] * 13,
        out_specs=[vmem] * 6,
        scratch_shapes=[pltpu.VMEM(a.shape, a.dtype) for a in small]
        + [
            pltpu.VMEM((6, 16, 16, D), BF16),
            pltpu.VMEM((2, 2, 16, D), BF16),
            pltpu.VMEM((2, 2, 16, D), BF16),
            pltpu.VMEM((2, 16, D), BF16),
            pltpu.VMEM((2, 2, 16, D), BF16),
            pltpu.VMEM((2 * WP, D), BF16),
            pltpu.VMEM((2 * WP, D), BF16),
            pltpu.VMEM((D, 2 * WP), BF16),
            pltpu.VMEM((D, 2 * WP), BF16),
            pltpu.VMEM((3, 256, 2 * WP), F32),
            pltpu.VMEM((2, 16, 8, WP), F32),
            pltpu.VMEM((256, 2 * WP), BF16),
            pltpu.VMEM((256, 2 * WP), BF16),
            pltpu.VMEM((256, WP), BF16),
            pltpu.VMEM((256, WP), BF16),
            pltpu.VMEM((2, NC, 128, CW), F32),
            pltpu.VMEM((4, NC, 128, CW), BF16),
            pltpu.VMEM((4, NC, 128, CW), BF16),
            pltpu.VMEM((4, 4, 2, NC, 16, CW), BF16),
            pltpu.VMEM((4, 2, 3, NC, 16, CW), BF16),
            pltpu.VMEM((4, 2, NC, 16, CW), BF16),
            pltpu.VMEM((4, 2, NC, 16, CW), BF16),
            pltpu.VMEM((2, 2, 16, D), F32),
            pltpu.VMEM((W, D), F32),
            pltpu.VMEM((W, D), F32),
            dma((9,)),
            dma((4,)),
            dma((6, 3, 2)),
            dma((6, 3, 2)),
            dma((6, 4, 2)),
            dma((6, 4, 2)),
            dma((4, NC)),
            dma((4, NC)),
            dma((4, 2, 3, NC)),
            dma((4, 2, 3, NC)),
            dma((4, 2, NC)),
            dma((4, 2, NC)),
            dma((2, 2)),
            dma((2, 3)),
            dma((2, 2)),
            dma((2, 3)),
            dma((2,)),
            dma((2,)),
        ],
        compiler_params=pltpu.CompilerParams(
            collective_id=0, has_side_effects=True, vmem_limit_bytes=54 * 1024 * 1024
        ),
    )(
        *small,
        up_weight[0].T, down_weight[0], up_dir[0].T, down_dir[0],
    )
    outs = pl.pallas_call(
        results,
        name="results",
        out_shape=(rows, rows, rows, rows, flat, flat),
        in_specs=[vmem] * 6,
        out_specs=[hbm] * 6,
        scratch_shapes=[dma((6,))],
    )(*[pltpu.with_memory_space_constraint(a, pltpu.VMEM) for a in outs])
    return outs[0], outs[1], outs[2], outs[3], outs[4].T[None], outs[5][None]


def solution(mesh):
    rows = P("section", "dp", None)
    in_specs = (
        rows, rows, rows, rows,
        P(None, "dp", None), P(None, "dp", None),
        P("section", None, "dp", None), P("section", None, "dp", None),
        P("section", None),
        P("section", None, "dp"), rows, P("section", None, "dp"), rows,
    )
    out_specs = (rows, rows, rows, rows, P("section", None, "dp"), rows)
    return jax.shard_map(shards, mesh=mesh, in_specs=in_specs, out_specs=out_specs, check_vma=False)
```

time: 114 us -> 94.3 us (0.83)
  Pallas kernels: 103 us -> 93.4 us
  local copies, waits for them, and re-layouts: 9.18 us -> 0 us
    pallas_call x1 -> x2, Pallas kernels: 103 us -> 93.4 us  [the longest x1 91.8 us: shards(): pl.pallas_call(kernel, name='relay', out_shape=[pltpu.VMEM(a.shape, a.dty...]
    unnamed x8 -> x0, local copies, waits for them, and re-layouts: 9.18 us -> none
where the time goes in v2:
time: 94.3 us; the launch traced here: 94.2 us
  Pallas kernels  93.4 us (99%)
    pallas_call x1, Pallas kernels, shards(): pl.pallas_call(kernel, name='relay', out_shape=[pltpu.VMEM(a.shape, a.dty...  91.8 us

profile of v2, /device:TPU:32, one launch (start us, length us, event | category | flops | bytes accessed | tf_op | source)
XLA Modules:
  0.0 94.2 jit_solution(3166800837265664675)
XLA Ops:
  0.6 91.8 %relay.1 = (bf16[1,8,2304]{2,1,0:T(8,128)(2,1)S(1)}, bf16[1,8,2304]{2,1,0:T(8,128)(2,1)S(1)}, bf16[1,8,2304]{2,1,0:T(8,128)(2,1)S(1)}, bf16[1,8,2304]{2,1,0:T(8,...) custom-call(bf16[1,8,2304]{2,1,0:T(8,128)(2,1)} %refs_0_.1, bf16[1,8,2304]{2,1,0:T(8,128)(2,1)} %refs_1_.1, ...), custom_call_target="tpu_custom_call" | custom-call | tf_op jit(solution)/shard_map/relay/pallas_call | solution.py:609
  92.4 1.6 %results.1 = (bf16[1,8,2304]{2,1,0:T(8,128)(2,1)}, bf16[1,8,2304]{2,1,0:T(8,128)(2,1)}, bf16[1,8,2304]{2,1,0:T(8,128)(2,1)}, bf16[1,8,2304]{2,1,0:T(8,128)(2,1)}...) custom-call(bf16[1,8,2304]{2,1,0:T(8,128)(2,1)S(1)} %get-tuple-element.18.refs_0_, ...), custom_call_target="tpu_custom_call" | custom-call | tf_op jit(solution)/shard_map/results/pallas_call | solution.py:668

commit v3 on v2

v3 whole, which is shorter than its diff:
```python
import jax
import jax.numpy as jnp
from jax import lax
from jax.experimental import pallas as pl
from jax.experimental.pallas import tpu as pltpu
from jax.sharding import PartitionSpec as P

MESH = pl.DeviceIdType.MESH
F32, BF16 = jnp.float32, jnp.bfloat16

ROOT = 0.7978845608028654
CUBIC = 0.044715
EPS = 1e-06

D = 2304
W = 288
WP = 384
NC = 3
CW = D // NC
M1, A1, N1, M2, A2, N2 = range(6)
RING = {M1: (1, 0), A1: (3, 0), N1: (1, 3), M2: (1, 3), A2: (0, 0), N2: (0, 0)}
T1, P1, T2, P2 = range(4)


def gelu_parts(v):
    u = ROOT * (v + CUBIC * v * v * v)
    s1 = ROOT * (1.0 + 3.0 * CUBIC * v * v)
    s2 = 6.0 * ROOT * CUBIC * v
    th = jnp.tanh(u)
    sech = 1.0 - th * th
    g0 = 0.5 * v * (1.0 + th)
    g1 = 0.5 * (1.0 + th) + 0.5 * v * sech * s1
    g2 = sech * (s1 - v * th * s1 * s1 + 0.5 * v * s2)
    return g0, g1, g2


def stats(r, rt):
    inv = lax.rsqrt(jnp.mean(r * r, axis=-1, keepdims=True) + EPS)
    inv_t = -(inv * inv * inv) * jnp.mean(r * rt, axis=-1, keepdims=True)
    return inv, inv_t


def norm_pair(block, gain):
    r, rt = block[:8], block[8:]
    inv, inv_t = stats(r, rt)
    return jnp.concatenate([r * inv * gain, (rt * inv + r * inv_t) * gain], axis=0).astype(BF16)


def norm_back(block, arriving, grads, gain):
    x, xt = block[:8], block[8:]
    inv, inv_t = stats(x, xt)
    w, wt = grads[:8] * gain, grads[8:] * gain
    mu = jnp.mean(x * w, axis=-1, keepdims=True)
    mu_t = jnp.mean(xt * w + x * wt, axis=-1, keepdims=True)
    cube = inv * inv * inv
    out = arriving[:8] + inv * w - cube * x * mu
    out_t = (
        arriving[8:]
        + inv_t * w
        + inv * wt
        - 3.0 * inv * inv * inv_t * x * mu
        - cube * xt * mu
        - cube * x * mu_t
    )
    return out, out_t


def kernel(*refs):
    up_h, down_h, upd_h, downd_h = refs[9:13]
    o_act, o_act_t, o_adj, o_adj_t, o_up, o_down = refs[13:19]
    small = c_act, c_act_t, c_adj, c_adj_t, fresh, loss, stash, stash_t, gain_ref = refs[19:28]
    G, ST, IN, CA, SH, WU, WV, WUT, WVT, AB, GL, XT, XP, QC, ZC, OWN, PS, PR, YS, YR, ZS, ZR, FB, CU, CD = refs[28:53]
    (i_sem, w_sem, lane_r, lane_s, part_r, part_s, pr_r, pr_s, yr_r, yr_s, zr_r, zr_s,
     in_r, in_s, ad_r, ad_s, st_r, st_s) = refs[53:]
    s, d = lax.axis_index("section"), lax.axis_index("dp")
    z, y, c = lax.div(d, 8), lax.rem(lax.div(d, 2), 4), lax.rem(d, 2)
    zo, co = 1 - z, 1 - c
    s_up, s_dn = lax.rem(s + 1, 16), lax.rem(s + 15, 16)

    def dev(ss, zz, yy, cc):
        return (ss, zz * 8 + yy * 2 + cc)

    def slot(cc, yy, zz):
        return zz * 8 + cc * 4 + yy

    ynb = [y, lax.rem(y + 1, 4), lax.rem(y + 2, 4), lax.rem(y + 3, 4)]
    ysrc = [y, ynb[3], ynb[2], ynb[1]]
    partner = dev(s, z, y, co)
    across = dev(s, zo, y, c)
    own = [slot(c, y, z), slot(c, y, zo)]
    zhs = [z, zo]

    firsts = [pltpu.make_async_copy(a, b, i_sem.at[i]) for i, (a, b) in enumerate(zip(refs[:9], small))]
    for i in (6, 7, 2, 3, 0, 1, 8, 4, 5):
        firsts[i].start()

    loads = []
    for i, (src, dst) in enumerate(((up_h, WU.at[pl.ds(0, W)]), (upd_h, WU.at[pl.ds(WP, W)]),
                                    (down_h, WV.at[pl.ds(0, W)]), (downd_h, WV.at[pl.ds(WP, W)]))):
        cp = pltpu.make_async_copy(src, dst, w_sem.at[i])
        cp.start()
        loads.append(cp)

    bar = pltpu.get_barrier_semaphore()
    peers = [partner, across] + [dev(s, z, ynb[i], c) for i in (1, 2, 3)]
    peers += [dev(ss, z, y, c) for ss in (s_up, s_dn)]
    for peer in peers:
        pl.semaphore_signal(bar, inc=1, device_id=peer, device_id_type=MESH)

    def put(src, dst, ssem, rsem, to):
        cp = pltpu.make_async_remote_copy(
            src_ref=src, dst_ref=dst, send_sem=ssem, recv_sem=rsem, device_id=to, device_id_type=MESH
        )
        cp.start()

    def got(dst, ssem, rsem):
        pltpu.make_async_remote_copy(
            src_ref=dst, dst_ref=dst, send_sem=ssem, recv_sem=rsem, device_id=partner, device_id_type=MESH
        ).wait_recv()

    def sent(src, ssem, rsem):
        pltpu.make_async_remote_copy(
            src_ref=src, dst_ref=src, send_sem=ssem, recv_sem=rsem, device_id=partner, device_id_type=MESH
        ).wait_send()

    def pair(a, b):
        return jnp.concatenate([a.astype(F32), b.astype(F32)], axis=0).astype(BF16)

    for cp in firsts:
        cp.wait()
    gain = gain_ref[...].astype(F32)

    CA[0] = pair(c_act[0], c_act_t[0])
    CA[1] = pair(c_adj[0], c_adj_t[0])
    for k in range(2):
        ST[k, z] = pair(stash[0, k], stash_t[0, k])

    pl.semaphore_wait(bar, 7)

    @pl.when(s != 0)
    def _():
        put(CA.at[1], G.at[A1, own[0]], ad_s.at[0, 0], ad_r.at[0, z], dev(s_dn, z, y, c))

    @pl.when(s != 15)
    def _():
        put(CA.at[0], IN.at[0, z], in_s.at[0, 0], in_r.at[0, z], dev(s_up, z, y, c))

    put(ST.at[0, z], ST.at[0, z], st_s.at[0], st_r.at[0], across)

    zero = jnp.zeros((8, D), F32)

    @pl.when(s == 0)
    def _():
        for k in range(2):
            IN[k, z] = pair(fresh[k], zero)

    @pl.when(s == 15)
    def _():
        for k, g in enumerate((A1, A2)):
            G[g, own[0]] = pair(loss[k], zero)

    def relay():
        ref = G.at[A1, own[0]]
        put(ref, ref, ad_s.at[0, 1], ad_r.at[0, z], across)

    def relay_in():
        ref = IN.at[0, z]
        put(ref, ref, in_s.at[0, 1], in_r.at[0, z], across)

    def relay_rest():
        put(ST.at[1, z], ST.at[1, z], st_s.at[1], st_r.at[1], across)

        @pl.when(s == 0)
        def _():
            put(IN.at[1, z], IN.at[1, z], in_s.at[1, 2], in_r.at[1, z], across)

        @pl.when(s == 15)
        def _():
            ref = G.at[A2, own[0]]
            put(ref, ref, ad_s.at[1, 2], ad_r.at[1, z], across)

    def wait_in(k, i, zz):
        def go():
            got(IN.at[k, zz], in_s.at[k, 0], in_r.at[k, zz])

        if k == 0 and i == 1:
            go()
        else:
            pl.when((s != 0) | (z != zz))(go)

    def wait_ad(k, i, zz):
        def go():
            ref = G.at[(A1, A2)[k], slot(c, y, zz)]
            got(ref, ad_s.at[k, 0], ad_r.at[k, zz])

        if k == 0 and i == 1:
            go()
        else:
            pl.when((s != 15) | (z != zz))(go)

    def send_own(g, i, zz):
        ref = G.at[g, slot(c, y, zz)]
        for dd in (1, 3) if RING[g][i] else (2, 1, 3):
            put(ref, ref, lane_s.at[g], lane_r.at[g, dd - 1, i], dev(s, z, ynb[dd], c))
        put(ref, ref, part_s.at[g], part_r.at[g, i], partner)

    def pass_on(g, i, zz, dds):
        for dd in dds:
            ref = G.at[g, slot(c, ysrc[dd], zz)]
            got(ref, lane_s.at[g], lane_r.at[g, dd - 1, i])
            if RING[g][i] == dd:
                put(ref, ref, lane_s.at[g], lane_r.at[g, 1, i], dev(s, z, ynb[dd], c))
            put(ref, ref, part_s.at[g], part_r.at[g, i], partner)

    def near(g, i, zz):
        pass_on(g, i, zz, (1, 3))

    def far(g, i, zz):
        pass_on(g, i, zz, (2,))

    def both(g, i, zz):
        pass_on(g, i, zz, (1, 3, 2))

    def finish(g, i, zz):
        got(G.at[g, pl.ds(slot(co, 0, zz), 4)], part_s.at[g], part_r.at[g, i])

    def norm_to(g, ref, zz):
        G[g, slot(c, y, zz)] = norm_pair(ref[zz].astype(F32), gain)

    def turn(weights, turned_weights):
        for j in range(9):
            cols = slice(j * 256, (j + 1) * 256)
            turned_weights[cols, :] = weights[:, cols].T

    def wide(n, g, weights, zz):
        x = G[g, pl.ds(8 * zz, 8)].reshape(128, D)
        for j in range(3):
            cols = slice(j * 256, (j + 1) * 256)
            AB[n, pl.ds(pl.multiple_of(128 * zz, 128), 128), cols] = jnp.dot(
                x, weights[:, cols], preferred_element_type=F32
            )

    def widened(n):
        r = AB[n].reshape(16, 16, 2 * WP)
        return r[:, :8, :WP], r[:, 8:, :WP] + r[:, :8, WP:]

    def left(X, v, vt):
        top = jnp.concatenate([v, jnp.zeros_like(v)], axis=2)
        low = jnp.concatenate([vt, v], axis=2)
        X[...] = jnp.concatenate([top, low], axis=1).reshape(256, 2 * WP).astype(BF16)

    def turned(v, vt):
        return jnp.concatenate([vt, v], axis=1).reshape(256, WP).astype(BF16)

    def lane(X, cc):
        return jnp.concatenate([X[pl.ds(pl.multiple_of(128 * h + 64 * cc, 64), 64), :] for h in range(2)], axis=0)

    def reduce_a(k, X, weights):
        for j in range(NC):
            wj = weights[:, j * CW : (j + 1) * CW]
            there = jnp.dot(lane(X, co), wj, preferred_element_type=F32)
            PS[k, j] = there.astype(BF16)
            put(PS.at[k, j], PR.at[k, j], pr_s.at[k], pr_r.at[k, j], partner)

    def reduce_b(k, X, weights, zz):
        for j in range(NC):
            wj = weights[:, j * CW : (j + 1) * CW]
            here = jnp.dot(lane(X, c), wj, preferred_element_type=F32)
            got(PR.at[k, j], pr_s.at[k], pr_r.at[k, j])
            total = here + PR[k, j].astype(F32)
            OWN[k % 2, j] = total
            YS[k, :, :, j] = total.astype(BF16).reshape(2, 4, 16, CW)
            reduce_y(k, 0, zz, j)

    def reduce_y(k, i, zz, j):
        for dd in (2, 1, 3):
            put(YS.at[k, zz, ynb[dd], j], YR.at[k, zz, j, dd - 1], yr_s.at[k], yr_r.at[k, i, j], dev(s, z, ynb[dd], c))

    def reduce_more(k, zz):
        for j in range(NC):
            reduce_y(k, 1, zz, j)

    def reduce_z(k, i, zz, chunks=range(NC)):
        for j in chunks:
            got(YR.at[k, zz, j], yr_s.at[k], yr_r.at[k, i, j])
            total = OWN[k % 2, j, pl.ds(pl.multiple_of(64 * zz + 16 * y, 16), 16), :]
            for dd in (1, 3, 2):
                total = total + YR[k, zz, j, dd - 1].astype(F32)
            if k < 2 or i == 0:
                ZS[k, zz, j] = total.astype(BF16)
                put(ZS.at[k, zz, j], ZR.at[k, zz, j], zr_s.at[k], zr_r.at[k, i, j], across)
            else:
                FB[k % 2, zz, :, j * CW : (j + 1) * CW] = total

    def reduce_end(k, i, zz):
        for j in range(NC):
            got(ZR.at[k, zz, j], zr_s.at[k], zr_r.at[k, i, j])
            cols = slice(j * CW, (j + 1) * CW)
            mine = ZS[k, zz, j].astype(F32) if k < 2 else FB[k % 2, zz, :, cols]
            FB[k % 2, zz, :, cols] = mine + ZR[k, zz, j].astype(F32)

    def forward_branch(tick):
        a, at = widened(0)
        g0, g1, _ = gelu_parts(a)
        left(XP, g0, g1 * at)
        reduce_a((P1, P2)[tick], XP, WV)

    def forward_rest(tick):
        reduce_b((P1, P2)[tick], XP, WV, (0, zo)[tick])

    def backward_first():
        b, bt = widened(1)
        g0, g1, g2 = gelu_parts(b)
        GL[0], GL[1] = g1, g2 * bt
        QC[...] = turned(g0, g1 * bt)

    def backward_second(tick):
        e, et = widened(2)
        zv, zt = e * GL[0], et * GL[0] + e * GL[1]
        left(XT, zv, zt)
        reduce_a((T1, T2)[tick], XT, WU)
        ZC[...] = turned(zv, zt)
        reduce_b((T1, T2)[tick], XT, WU, (0, zo)[tick])

    def curvature(tick, which):
        for lhs, acc, g, o in (((QC, CD, (A1, A2)[tick], 1), (ZC, CU, (M1, M2)[tick], 0))[which],):
            lt = lhs[...].T[:W]
            x = G[g].reshape(256, D)
            for j in range(NC):
                cols = slice(j * CW, (j + 1) * CW)
                part = jnp.dot(lt, x[:, cols], preferred_element_type=F32)
                if tick == 0:
                    acc[:, cols] = part
                else:
                    (o_up, o_down)[o][:, cols] = (acc[:, cols] + part).astype(BF16)

    def next_adjoint(zz):
        out, out_t = norm_back(ST[0, zz].astype(F32), G[A1, slot(c, y, zz)].astype(F32), FB[0, zz], gain)
        SH[0, zz] = jnp.concatenate([out, out_t], axis=0).astype(BF16)

        @pl.when(s != 0)
        def _():
            put(SH.at[0, zz], G.at[A2, slot(c, y, zz)], ad_s.at[1, zz], ad_r.at[1, zz], dev(s_dn, z, y, c))

    def next_input(zz):
        SH[1, zz] = (IN[0, zz].astype(F32) + FB[1, zz]).astype(BF16)

        @pl.when(s != 15)
        def _():
            put(SH.at[1, zz], IN.at[1, zz], in_s.at[1, zz], in_r.at[1, zz], dev(s_up, z, y, c))

    def settle_edges():
        sent(CA.at[0], ad_s.at[0, 1], ad_r.at[0, z])
        sent(CA.at[0], in_s.at[0, 1], in_r.at[0, z])

        @pl.when(s != 0)
        def _():
            sent(CA.at[1], ad_s.at[0, 0], ad_r.at[0, z])
            for i in range(2):
                sent(SH.at[0, i], ad_s.at[1, i], ad_r.at[1, z])

        @pl.when(s != 15)
        def _():
            sent(CA.at[0], in_s.at[0, 0], in_r.at[0, z])
            for i in range(2):
                sent(SH.at[1, i], in_s.at[1, i], in_r.at[1, z])

        @pl.when(s == 0)
        def _():
            sent(IN.at[1, z], in_s.at[1, 2], in_r.at[1, z])

        @pl.when(s == 15)
        def _():
            sent(G.at[A2, own[0]], ad_s.at[1, 2], ad_r.at[1, z])

    norm_to(M1, ST.at[0], z)
    send_own(M1, 0, z)
    norm_to(M2, ST.at[1], z)
    send_own(M2, 0, z)
    for r in range(2):
        WU[r * WP + W : (r + 1) * WP, :] = jnp.zeros((WP - W, D), BF16)
        WV[r * WP + W : (r + 1) * WP, :] = jnp.zeros((WP - W, D), BF16)
    wait_ad(0, 0, z)
    relay()
    send_own(A1, 0, z)
    wait_in(0, 0, z)
    relay_in()
    relay_rest()
    near(M1, 0, z)
    for cp in loads:
        cp.wait()
    turn(WU, WUT)
    got(ST.at[0, zo], st_s.at[0], st_r.at[0])
    norm_to(M1, ST.at[0], zo)
    send_own(M1, 1, zo)
    near(A1, 0, z)
    turn(WV, WVT)
    norm_to(N1, IN.at[0], z)
    wait_ad(0, 1, zo)
    send_own(A1, 1, zo)
    send_own(N1, 0, z)
    near(M2, 0, z)
    far(M1, 0, z)
    far(A1, 0, z)
    finish(M1, 0, z)
    wide(1, M1, WUT, z)
    both(M1, 1, zo)
    wait_in(0, 1, zo)
    norm_to(N1, IN.at[0], zo)
    send_own(N1, 1, zo)
    finish(A1, 0, z)
    wide(2, A1, WVT, z)
    finish(M1, 1, zo)
    wide(1, M1, WUT, zo)
    backward_first()
    both(A1, 1, zo)
    near(N1, 0, z)
    got(ST.at[1, zo], st_s.at[1], st_r.at[1])
    norm_to(M2, ST.at[1], zo)
    send_own(M2, 1, zo)
    finish(A1, 1, zo)
    wide(2, A1, WVT, zo)
    near(N1, 1, zo)
    backward_second(0)
    reduce_more(T1, 1)
    far(N1, 0, z)
    far(N1, 1, zo)
    near(M2, 1, zo)
    finish(N1, 0, z)
    wide(0, N1, WUT, z)
    reduce_z(T1, 0, 0, (0,))
    finish(N1, 1, zo)
    wide(0, N1, WUT, zo)
    reduce_z(T1, 0, 0, (1,))
    forward_branch(0)
    reduce_z(T1, 0, 0, (2,))
    forward_rest(0)
    reduce_more(P1, 1)
    reduce_z(T1, 1, 1)
    far(M2, 0, z)
    curvature(0, 0)
    reduce_end(T1, 0, 0)
    next_adjoint(0)
    reduce_z(P1, 0, 0)
    curvature(0, 1)
    reduce_end(T1, 1, 1)
    next_adjoint(1)
    wait_ad(1, 0, 0)
    send_own(A2, 0, 0)
    far(M2, 1, zo)
    reduce_z(P1, 1, 1)
    finish(M2, 0, z)
    wide(1, M2, WUT, z)
    wait_ad(1, 1, 1)
    send_own(A2, 1, 1)
    reduce_end(P1, 0, 0)
    next_input(0)
    finish(M2, 1, zo)
    wide(1, M2, WUT, zo)
    backward_first()
    both(A2, 0, 0)
    reduce_end(P1, 1, 1)
    next_input(1)
    finish(A2, 0, 0)
    wide(2, A2, WVT, 0)
    wait_in(1, 0, 0)
    norm_to(N2, IN.at[1], 0)
    send_own(N2, 0, 0)
    both(A2, 1, 1)
    wait_in(1, 1, 1)
    norm_to(N2, IN.at[1], 1)
    send_own(N2, 1, 1)
    finish(A2, 1, 1)
    wide(2, A2, WVT, 1)
    backward_second(1)
    reduce_more(T2, z)
    both(N2, 0, 0)
    finish(N2, 0, 0)
    wide(0, N2, WUT, 0)
    both(N2, 1, 1)
    finish(N2, 1, 1)
    wide(0, N2, WUT, 1)
    forward_branch(1)
    forward_rest(1)
    reduce_more(P2, z)
    reduce_z(T2, 0, zo)
    curvature(1, 0)
    curvature(1, 1)
    settle_edges()
    reduce_z(T2, 1, z)
    reduce_z(P2, 0, zo)
    reduce_end(T2, 0, z)
    out, out_t = norm_back(ST[1, z].astype(F32), G[A2, own[0]].astype(F32), FB[0, z], gain)
    o_adj[0] = out.astype(BF16)
    o_adj_t[0] = out_t.astype(BF16)
    reduce_z(P2, 1, z)
    reduce_end(P2, 0, z)
    result = IN[1, z].astype(F32) + FB[1, z]
    o_act[0] = result[:8].astype(BF16)
    o_act_t[0] = result[8:].astype(BF16)

    for g in range(6):
        sent(G.at[g, pl.ds(0, 6)], lane_s.at[g], part_r.at[g, 0])
        sent(G.at[g, pl.ds(0, 8)], part_s.at[g], part_r.at[g, 0])
    for k in range(4):
        sent(PS.at[k], pr_s.at[k], pr_r.at[k, 0])
        sent(YS.at[k, :, pl.ds(0, 3)], yr_s.at[k], pr_r.at[k, 0])
        sent(ZS.at[k] if k < 2 else ZS.at[k, 0], zr_s.at[k], pr_r.at[k, 0])
    for k in range(2):
        sent(ST.at[k, z], st_s.at[k], st_r.at[k])


def results(*refs):
    srcs, dsts, sem = refs[:6], refs[6:12], refs[12]
    copies = [pltpu.make_async_copy(a, b, sem.at[i]) for i, (a, b) in enumerate(zip(srcs, dsts))]
    for cp in copies:
        cp.start()
    for cp in copies:
        cp.wait()


def shards(
    carry_act, carry_act_tan, carry_adj, carry_adj_tan, fresh_act, loss_cot, stash_act, stash_act_tan,
    norm_gain, up_weight, down_weight, up_dir, down_dir,
):
    rows = jax.ShapeDtypeStruct((1, 8, D), BF16)
    flat = jax.ShapeDtypeStruct((W, D), BF16)
    vmem, hbm = pl.BlockSpec(memory_space=pltpu.VMEM), pl.BlockSpec(memory_space=pl.ANY)
    dma = pltpu.SemaphoreType.DMA
    small = (
        carry_act, carry_act_tan, carry_adj, carry_adj_tan, fresh_act, loss_cot, stash_act, stash_act_tan, norm_gain,
    )
    outs = pl.pallas_call(
        kernel,
        name="relay",
        out_shape=[pltpu.VMEM(a.shape, a.dtype) for a in (rows, rows, rows, rows, flat, flat)],
        in_specs=[pl.BlockSpec(memory_space=pltpu.HBM)] * 13,
        out_specs=[vmem] * 6,
        scratch_shapes=[pltpu.VMEM(a.shape, a.dtype) for a in small]
        + [
            pltpu.VMEM((6, 16, 16, D), BF16),
            pltpu.VMEM((2, 2, 16, D), BF16),
            pltpu.VMEM((2, 2, 16, D), BF16),
            pltpu.VMEM((2, 16, D), BF16),
            pltpu.VMEM((2, 2, 16, D), BF16),
            pltpu.VMEM((2 * WP, D), BF16),
            pltpu.VMEM((2 * WP, D), BF16),
            pltpu.VMEM((D, 2 * WP), BF16),
            pltpu.VMEM((D, 2 * WP), BF16),
            pltpu.VMEM((3, 256, 2 * WP), F32),
            pltpu.VMEM((2, 16, 8, WP), F32),
            pltpu.VMEM((256, 2 * WP), BF16),
            pltpu.VMEM((256, 2 * WP), BF16),
            pltpu.VMEM((256, WP), BF16),
            pltpu.VMEM((256, WP), BF16),
            pltpu.VMEM((2, NC, 128, CW), F32),
            pltpu.VMEM((4, NC, 128, CW), BF16),
            pltpu.VMEM((4, NC, 128, CW), BF16),
            pltpu.VMEM((4, 2, 4, NC, 16, CW), BF16),
            pltpu.VMEM((4, 2, NC, 3, 16, CW), BF16),
            pltpu.VMEM((4, 2, NC, 16, CW), BF16),
            pltpu.VMEM((4, 2, NC, 16, CW), BF16),
            pltpu.VMEM((2, 2, 16, D), F32),
            pltpu.VMEM((W, D), F32),
            pltpu.VMEM((W, D), F32),
            dma((9,)),
            dma((4,)),
            dma((6, 3, 2)),
            dma((6,)),
            dma((6, 2)),
            dma((6,)),
            dma((4, NC)),
            dma((4,)),
            dma((4, 2, NC)),
            dma((4,)),
            dma((4, 2, NC)),
            dma((4,)),
            dma((2, 2)),
            dma((2, 3)),
            dma((2, 2)),
            dma((2, 3)),
            dma((2,)),
            dma((2,)),
        ],
        compiler_params=pltpu.CompilerParams(
            collective_id=0, has_side_effects=True, vmem_limit_bytes=54 * 1024 * 1024
        ),
    )(
        *small,
        up_weight[0].T, down_weight[0], up_dir[0].T, down_dir[0],
    )
    outs = pl.pallas_call(
        results,
        name="results",
        out_shape=(rows, rows, rows, rows, flat, flat),
        in_specs=[vmem] * 6,
        out_specs=[hbm] * 6,
        scratch_shapes=[dma((6,))],
    )(*[pltpu.with_memory_space_constraint(a, pltpu.VMEM) for a in outs])
    return outs[0], outs[1], outs[2], outs[3], outs[4].T[None], outs[5][None]


def solution(mesh):
    rows = P("section", "dp", None)
    in_specs = (
        rows, rows, rows, rows,
        P(None, "dp", None), P(None, "dp", None),
        P("section", None, "dp", None), P("section", None, "dp", None),
        P("section", None),
        P("section", None, "dp"), rows, P("section", None, "dp"), rows,
    )
    out_specs = (rows, rows, rows, rows, P("section", None, "dp"), rows)
    return jax.shard_map(shards, mesh=mesh, in_specs=in_specs, out_specs=out_specs, check_vma=False)
```

time: 94.3 us -> 87.9 us (0.932)
  Pallas kernels: 93.4 us -> 87 us
    pallas_call x1, Pallas kernels: 91.8 us -> 85.4 us  [shards(): pl.pallas_call(kernel, name='relay', out_shape=[pltpu.VMEM(a.shape, a.dty...]
where the time goes in v3:
time: 87.9 us; the launch traced here: 87.8 us
  Pallas kernels  87 us (99%)
    pallas_call x1, Pallas kernels, shards(): pl.pallas_call(kernel, name='relay', out_shape=[pltpu.VMEM(a.shape, a.dty...  85.4 us

profile of v3, /device:TPU:32, one launch (start us, length us, event | category | flops | bytes accessed | tf_op | source)
XLA Modules:
  0.0 87.8 jit_solution(9371117420582535901)
XLA Ops:
  0.6 85.4 %relay.1 = (bf16[1,8,2304]{2,1,0:T(8,128)(2,1)S(1)}, bf16[1,8,2304]{2,1,0:T(8,128)(2,1)S(1)}, bf16[1,8,2304]{2,1,0:T(8,128)(2,1)S(1)}, bf16[1,8,2304]{2,1,0:T(8,...) custom-call(bf16[1,8,2304]{2,1,0:T(8,128)(2,1)} %refs_0_.1, bf16[1,8,2304]{2,1,0:T(8,128)(2,1)} %refs_1_.1, ...), custom_call_target="tpu_custom_call" | custom-call | tf_op jit(solution)/shard_map/relay/pallas_call | solution.py:533
  86.0 1.6 %results.1 = (bf16[1,8,2304]{2,1,0:T(8,128)(2,1)}, bf16[1,8,2304]{2,1,0:T(8,128)(2,1)}, bf16[1,8,2304]{2,1,0:T(8,128)(2,1)}, bf16[1,8,2304]{2,1,0:T(8,128)(2,1)}...) custom-call(bf16[1,8,2304]{2,1,0:T(8,128)(2,1)S(1)} %get-tuple-element.18.refs_0_, ...), custom_call_target="tpu_custom_call" | custom-call | tf_op jit(solution)/shard_map/results/pallas_call | solution.py:592

commit v4 on v3

--- a/solution.py
+++ b/solution.py
@@ -18,7 +18,7 @@
 NC = 3
 CW = D // NC
 M1, A1, N1, M2, A2, N2 = range(6)
-RING = {M1: (1, 0), A1: (3, 0), N1: (1, 3), M2: (1, 3), A2: (0, 0), N2: (0, 0)}
+RING = {M1: (1, 0), A1: (3, 0), N1: (1, 3), M2: (1, 0), A2: (0, 0), N2: (0, 0)}
 T1, P1, T2, P2 = range(4)
 
 
@@ -71,7 +71,7 @@
     small = c_act, c_act_t, c_adj, c_adj_t, fresh, loss, stash, stash_t, gain_ref = refs[19:28]
     G, ST, IN, CA, SH, WU, WV, WUT, WVT, AB, GL, XT, XP, QC, ZC, OWN, PS, PR, YS, YR, ZS, ZR, FB, CU, CD = refs[28:53]
     (i_sem, w_sem, lane_r, lane_s, part_r, part_s, pr_r, pr_s, yr_r, yr_s, zr_r, zr_s,
-     in_r, in_s, ad_r, ad_s, st_r, st_s) = refs[53:]
+     in_r, in_s, ad_r, ad_s, st_r, st_s, next_r) = refs[53:]
     s, d = lax.axis_index("section"), lax.axis_index("dp")
     z, y, c = lax.div(d, 8), lax.rem(lax.div(d, 2), 4), lax.rem(d, 2)
     zo, co = 1 - z, 1 - c
@@ -172,7 +172,9 @@
 
         @pl.when(s == 0)
         def _():
-            put(IN.at[1, z], IN.at[1, z], in_s.at[1, 2], in_r.at[1, z], across)
+            for j in range(NC):
+                ref = IN.at[1, z, :, j * CW : (j + 1) * CW]
+                put(ref, ref, in_s.at[1, 2], next_r.at[z, j], across)
 
         @pl.when(s == 15)
         def _():
@@ -181,7 +183,11 @@
 
     def wait_in(k, i, zz):
         def go():
-            got(IN.at[k, zz], in_s.at[k, 0], in_r.at[k, zz])
+            if k == 0:
+                got(IN.at[0, zz], in_s.at[0, 0], in_r.at[0, zz])
+            else:
+                for j in range(NC):
+                    got(IN.at[1, zz, :, j * CW : (j + 1) * CW], in_s.at[1, 0], next_r.at[zz, j])
 
         if k == 0 and i == 1:
             go()
@@ -292,8 +298,8 @@
             else:
                 FB[k % 2, zz, :, j * CW : (j + 1) * CW] = total
 
-    def reduce_end(k, i, zz):
-        for j in range(NC):
+    def reduce_end(k, i, zz, chunks=range(NC)):
+        for j in chunks:
             got(ZR.at[k, zz, j], zr_s.at[k], zr_r.at[k, i, j])
             cols = slice(j * CW, (j + 1) * CW)
             mine = ZS[k, zz, j].astype(F32) if k < 2 else FB[k % 2, zz, :, cols]
@@ -343,11 +349,14 @@
             put(SH.at[0, zz], G.at[A2, slot(c, y, zz)], ad_s.at[1, zz], ad_r.at[1, zz], dev(s_dn, z, y, c))
 
     def next_input(zz):
-        SH[1, zz] = (IN[0, zz].astype(F32) + FB[1, zz]).astype(BF16)
-
-        @pl.when(s != 15)
-        def _():
-            put(SH.at[1, zz], IN.at[1, zz], in_s.at[1, zz], in_r.at[1, zz], dev(s_up, z, y, c))
+        for j in range(NC):
+            cols = slice(j * CW, (j + 1) * CW)
+            reduce_end(P1, zz, zz, (j,))
+            SH[1, zz, :, cols] = (IN[0, zz, :, cols].astype(F32) + FB[1, zz, :, cols]).astype(BF16)
+
+            @pl.when(s != 15)
+            def _():
+                put(SH.at[1, zz, :, cols], IN.at[1, zz, :, cols], in_s.at[1, zz], next_r.at[zz, j], dev(s_up, z, y, c))
 
     def settle_edges():
         sent(CA.at[0], ad_s.at[0, 1], ad_r.at[0, z])
@@ -363,11 +372,11 @@
         def _():
             sent(CA.at[0], in_s.at[0, 0], in_r.at[0, z])
             for i in range(2):
-                sent(SH.at[1, i], in_s.at[1, i], in_r.at[1, z])
+                sent(SH.at[1, i], in_s.at[1, i], in_r.at[0, z])
 
         @pl.when(s == 0)
         def _():
-            sent(IN.at[1, z], in_s.at[1, 2], in_r.at[1, z])
+            sent(IN.at[1, z], in_s.at[1, 2], in_r.at[0, z])
 
         @pl.when(s == 15)
         def _():
@@ -399,7 +408,6 @@
     wait_ad(0, 1, zo)
     send_own(A1, 1, zo)
     send_own(N1, 0, z)
-    near(M2, 0, z)
     far(M1, 0, z)
     far(A1, 0, z)
     finish(M1, 0, z)
@@ -415,9 +423,6 @@
     backward_first()
     both(A1, 1, zo)
     near(N1, 0, z)
-    got(ST.at[1, zo], st_s.at[1], st_r.at[1])
-    norm_to(M2, ST.at[1], zo)
-    send_own(M2, 1, zo)
     finish(A1, 1, zo)
     wide(2, A1, WVT, zo)
     near(N1, 1, zo)
@@ -425,7 +430,8 @@
     reduce_more(T1, 1)
     far(N1, 0, z)
     far(N1, 1, zo)
-    near(M2, 1, zo)
+    got(ST.at[1, zo], st_s.at[1], st_r.at[1])
+    norm_to(M2, ST.at[1], zo)
     finish(N1, 0, z)
     wide(0, N1, WUT, z)
     reduce_z(T1, 0, 0, (0,))
@@ -436,8 +442,9 @@
     reduce_z(T1, 0, 0, (2,))
     forward_rest(0)
     reduce_more(P1, 1)
+    near(M2, 0, z)
+    send_own(M2, 1, zo)
     reduce_z(T1, 1, 1)
-    far(M2, 0, z)
     curvature(0, 0)
     reduce_end(T1, 0, 0)
     next_adjoint(0)
@@ -445,27 +452,26 @@
     curvature(0, 1)
     reduce_end(T1, 1, 1)
     next_adjoint(1)
+    reduce_z(P1, 1, 1)
     wait_ad(1, 0, 0)
     send_own(A2, 0, 0)
-    far(M2, 1, zo)
-    reduce_z(P1, 1, 1)
+    far(M2, 0, z)
     finish(M2, 0, z)
     wide(1, M2, WUT, z)
+    next_input(0)
     wait_ad(1, 1, 1)
     send_own(A2, 1, 1)
-    reduce_end(P1, 0, 0)
-    next_input(0)
+    both(M2, 1, zo)
+    next_input(1)
     finish(M2, 1, zo)
     wide(1, M2, WUT, zo)
+    both(A2, 0, 0)
     backward_first()
-    both(A2, 0, 0)
-    reduce_end(P1, 1, 1)
-    next_input(1)
-    finish(A2, 0, 0)
-    wide(2, A2, WVT, 0)
     wait_in(1, 0, 0)
     norm_to(N2, IN.at[1], 0)
     send_own(N2, 0, 0)
+    finish(A2, 0, 0)
+    wide(2, A2, WVT, 0)
     both(A2, 1, 1)
     wait_in(1, 1, 1)
     norm_to(N2, IN.at[1], 1)
@@ -475,19 +481,19 @@
     backward_second(1)
     reduce_more(T2, z)
     both(N2, 0, 0)
+    both(N2, 1, 1)
     finish(N2, 0, 0)
     wide(0, N2, WUT, 0)
-    both(N2, 1, 1)
     finish(N2, 1, 1)
     wide(0, N2, WUT, 1)
     forward_branch(1)
     forward_rest(1)
     reduce_more(P2, z)
     reduce_z(T2, 0, zo)
+    reduce_z(T2, 1, z)
     curvature(1, 0)
     curvature(1, 1)
     settle_edges()
-    reduce_z(T2, 1, z)
     reduce_z(P2, 0, zo)
     reduce_end(T2, 0, z)
     out, out_t = norm_back(ST[1, z].astype(F32), G[A2, own[0]].astype(F32), FB[0, z], gain)
@@ -575,12 +581,13 @@
             dma((4,)),
             dma((4, 2, NC)),
             dma((4,)),
-            dma((2, 2)),
+            dma((1, 2)),
             dma((2, 3)),
             dma((2, 2)),
             dma((2, 3)),
             dma((2,)),
             dma((2,)),
+            dma((2, NC)),
         ],
         compiler_params=pltpu.CompilerParams(
             collective_id=0, has_side_effects=True, vmem_limit_bytes=54 * 1024 * 1024

time: 87.9 us -> 85.5 us (0.973)
  Pallas kernels: 87 us -> 84.7 us
    pallas_call x1, Pallas kernels: 85.4 us -> 83 us  [shards(): pl.pallas_call(kernel, name='relay', out_shape=[pltpu.VMEM(a.shape, a.dty...]
where the time goes in v4:
time: 85.5 us
  Pallas kernels  84.7 us (99%)
    pallas_call x1, Pallas kernels, shards(): pl.pallas_call(kernel, name='relay', out_shape=[pltpu.VMEM(a.shape, a.dty...  83 us

profile of v4, /device:TPU:32, one launch (start us, length us, event | category | flops | bytes accessed | tf_op | source)
XLA Modules:
  0.0 85.5 jit_solution(6592260291383001320)
XLA Ops:
  0.6 83.0 %relay.1 = (bf16[1,8,2304]{2,1,0:T(8,128)(2,1)S(1)}, bf16[1,8,2304]{2,1,0:T(8,128)(2,1)S(1)}, bf16[1,8,2304]{2,1,0:T(8,128)(2,1)S(1)}, bf16[1,8,2304]{2,1,0:T(8,...) custom-call(bf16[1,8,2304]{2,1,0:T(8,128)(2,1)} %refs_0_.1, bf16[1,8,2304]{2,1,0:T(8,128)(2,1)} %refs_1_.1, ...), custom_call_target="tpu_custom_call" | custom-call | tf_op jit(solution)/shard_map/relay/pallas_call | solution.py:539
  83.7 1.6 %results.1 = (bf16[1,8,2304]{2,1,0:T(8,128)(2,1)}, bf16[1,8,2304]{2,1,0:T(8,128)(2,1)}, bf16[1,8,2304]{2,1,0:T(8,128)(2,1)}, bf16[1,8,2304]{2,1,0:T(8,128)(2,1)}...) custom-call(bf16[1,8,2304]{2,1,0:T(8,128)(2,1)S(1)} %get-tuple-element.18.refs_0_, ...), custom_call_target="tpu_custom_call" | custom-call | tf_op jit(solution)/shard_map/results/pallas_call | solution.py:599

commit v5 on v4

--- a/solution.py
+++ b/solution.py
@@ -90,6 +90,12 @@
     own = [slot(c, y, z), slot(c, y, zo)]
     zhs = [z, zo]
 
+    bar = pltpu.get_barrier_semaphore()
+    peers = [partner, across] + [dev(s, z, ynb[i], c) for i in (1, 2, 3)]
+    peers += [dev(ss, z, y, c) for ss in (s_up, s_dn)]
+    for peer in peers:
+        pl.semaphore_signal(bar, inc=1, device_id=peer, device_id_type=MESH)
+
     firsts = [pltpu.make_async_copy(a, b, i_sem.at[i]) for i, (a, b) in enumerate(zip(refs[:9], small))]
     for i in (6, 7, 2, 3, 0, 1, 8, 4, 5):
         firsts[i].start()
@@ -100,12 +106,6 @@
         cp = pltpu.make_async_copy(src, dst, w_sem.at[i])
         cp.start()
         loads.append(cp)
-
-    bar = pltpu.get_barrier_semaphore()
-    peers = [partner, across] + [dev(s, z, ynb[i], c) for i in (1, 2, 3)]
-    peers += [dev(ss, z, y, c) for ss in (s_up, s_dn)]
-    for peer in peers:
-        pl.semaphore_signal(bar, inc=1, device_id=peer, device_id_type=MESH)
 
     def put(src, dst, ssem, rsem, to):
         cp = pltpu.make_async_remote_copy(
@@ -207,16 +207,16 @@
     def send_own(g, i, zz):
         ref = G.at[g, slot(c, y, zz)]
         for dd in (1, 3) if RING[g][i] else (2, 1, 3):
-            put(ref, ref, lane_s.at[g], lane_r.at[g, dd - 1, i], dev(s, z, ynb[dd], c))
-        put(ref, ref, part_s.at[g], part_r.at[g, i], partner)
+            put(ref, ref, lane_s.at[0], lane_r.at[g, dd - 1, i], dev(s, z, ynb[dd], c))
+        put(ref, ref, part_s.at[0], part_r.at[g, i], partner)
 
     def pass_on(g, i, zz, dds):
         for dd in dds:
             ref = G.at[g, slot(c, ysrc[dd], zz)]
-            got(ref, lane_s.at[g], lane_r.at[g, dd - 1, i])
+            got(ref, lane_s.at[0], lane_r.at[g, dd - 1, i])
             if RING[g][i] == dd:
-                put(ref, ref, lane_s.at[g], lane_r.at[g, 1, i], dev(s, z, ynb[dd], c))
-            put(ref, ref, part_s.at[g], part_r.at[g, i], partner)
+                put(ref, ref, lane_s.at[0], lane_r.at[g, 1, i], dev(s, z, ynb[dd], c))
+            put(ref, ref, part_s.at[0], part_r.at[g, i], partner)
 
     def near(g, i, zz):
         pass_on(g, i, zz, (1, 3))
@@ -228,7 +228,7 @@
         pass_on(g, i, zz, (1, 3, 2))
 
     def finish(g, i, zz):
-        got(G.at[g, pl.ds(slot(co, 0, zz), 4)], part_s.at[g], part_r.at[g, i])
+        got(G.at[g, pl.ds(slot(co, 0, zz), 4)], part_s.at[0], part_r.at[g, i])
 
     def norm_to(g, ref, zz):
         G[g, slot(c, y, zz)] = norm_pair(ref[zz].astype(F32), gain)
@@ -266,13 +266,13 @@
             wj = weights[:, j * CW : (j + 1) * CW]
             there = jnp.dot(lane(X, co), wj, preferred_element_type=F32)
             PS[k, j] = there.astype(BF16)
-            put(PS.at[k, j], PR.at[k, j], pr_s.at[k], pr_r.at[k, j], partner)
+            put(PS.at[k, j], PR.at[k, j], pr_s.at[0], pr_r.at[k, j], partner)
 
     def reduce_b(k, X, weights, zz):
         for j in range(NC):
             wj = weights[:, j * CW : (j + 1) * CW]
             here = jnp.dot(lane(X, c), wj, preferred_element_type=F32)
-            got(PR.at[k, j], pr_s.at[k], pr_r.at[k, j])
+            got(PR.at[k, j], pr_s.at[0], pr_r.at[k, j])
             total = here + PR[k, j].astype(F32)
             OWN[k % 2, j] = total
             YS[k, :, :, j] = total.astype(BF16).reshape(2, 4, 16, CW)
@@ -280,7 +280,7 @@
 
     def reduce_y(k, i, zz, j):
         for dd in (2, 1, 3):
-            put(YS.at[k, zz, ynb[dd], j], YR.at[k, zz, j, dd - 1], yr_s.at[k], yr_r.at[k, i, j], dev(s, z, ynb[dd], c))
+            put(YS.at[k, zz, ynb[dd], j], YR.at[k, zz, j, dd - 1], yr_s.at[0], yr_r.at[k, i, j], dev(s, z, ynb[dd], c))
 
     def reduce_more(k, zz):
         for j in range(NC):
@@ -288,19 +288,19 @@
 
     def reduce_z(k, i, zz, chunks=range(NC)):
         for j in chunks:
-            got(YR.at[k, zz, j], yr_s.at[k], yr_r.at[k, i, j])
+            got(YR.at[k, zz, j], yr_s.at[0], yr_r.at[k, i, j])
             total = OWN[k % 2, j, pl.ds(pl.multiple_of(64 * zz + 16 * y, 16), 16), :]
             for dd in (1, 3, 2):
                 total = total + YR[k, zz, j, dd - 1].astype(F32)
             if k < 2 or i == 0:
                 ZS[k, zz, j] = total.astype(BF16)
-                put(ZS.at[k, zz, j], ZR.at[k, zz, j], zr_s.at[k], zr_r.at[k, i, j], across)
+                put(ZS.at[k, zz, j], ZR.at[k, zz, j], zr_s.at[0], zr_r.at[(k * 2 + i if k < 2 else k + 2) * NC + j], across)
             else:
                 FB[k % 2, zz, :, j * CW : (j + 1) * CW] = total
 
     def reduce_end(k, i, zz, chunks=range(NC)):
         for j in chunks:
-            got(ZR.at[k, zz, j], zr_s.at[k], zr_r.at[k, i, j])
+            got(ZR.at[k, zz, j], zr_s.at[0], zr_r.at[(k * 2 + i if k < 2 else k + 2) * NC + j])
             cols = slice(j * CW, (j + 1) * CW)
             mine = ZS[k, zz, j].astype(F32) if k < 2 else FB[k % 2, zz, :, cols]
             FB[k % 2, zz, :, cols] = mine + ZR[k, zz, j].astype(F32)
@@ -505,13 +505,11 @@
     o_act[0] = result[:8].astype(BF16)
     o_act_t[0] = result[8:].astype(BF16)
 
-    for g in range(6):
-        sent(G.at[g, pl.ds(0, 6)], lane_s.at[g], part_r.at[g, 0])
-        sent(G.at[g, pl.ds(0, 8)], part_s.at[g], part_r.at[g, 0])
-    for k in range(4):
-        sent(PS.at[k], pr_s.at[k], pr_r.at[k, 0])
-        sent(YS.at[k, :, pl.ds(0, 3)], yr_s.at[k], pr_r.at[k, 0])
-        sent(ZS.at[k] if k < 2 else ZS.at[k, 0], zr_s.at[k], pr_r.at[k, 0])
+    sent(G.at[pl.ds(0, 3), pl.ds(0, 12)], lane_s.at[0], part_r.at[0, 0])
+    sent(G.at[pl.ds(0, 3)], part_s.at[0], part_r.at[0, 0])
+    sent(PS, pr_s.at[0], part_r.at[0, 0])
+    sent(YS.at[:, :, pl.ds(0, 3)], yr_s.at[0], part_r.at[0, 0])
+    sent(ZS.at[pl.ds(0, 3)], zr_s.at[0], part_r.at[0, 0])
     for k in range(2):
         sent(ST.at[k, z], st_s.at[k], st_r.at[k])
 
@@ -572,15 +570,15 @@
             dma((9,)),
             dma((4,)),
             dma((6, 3, 2)),
-            dma((6,)),
+            dma((1,)),
             dma((6, 2)),
-            dma((6,)),
+            dma((1,)),
             dma((4, NC)),
-            dma((4,)),
+            dma((1,)),
             dma((4, 2, NC)),
-            dma((4,)),
-            dma((4, 2, NC)),
-            dma((4,)),
+            dma((1,)),
+            dma((6 * NC,)),
+            dma((1,)),
             dma((1, 2)),
             dma((2, 3)),
             dma((2, 2)),

time: 85.5 us -> 85.6 us (level)
  no operation moved by 1% of the time
where the time goes in v5:
time: 85.6 us; the launch traced here: 85.5 us
  Pallas kernels  84.7 us (99%)
    pallas_call x1, Pallas kernels, shards(): pl.pallas_call(kernel, name='relay', out_shape=[pltpu.VMEM(a.shape, a.dty...  83.1 us

profile of v5, /device:TPU:32, one launch (start us, length us, event | category | flops | bytes accessed | tf_op | source)
XLA Modules:
  0.0 85.5 jit_solution(14583270583973424655)
XLA Ops:
  0.6 83.1 %relay.1 = (bf16[1,8,2304]{2,1,0:T(8,128)(2,1)S(1)}, bf16[1,8,2304]{2,1,0:T(8,128)(2,1)S(1)}, bf16[1,8,2304]{2,1,0:T(8,128)(2,1)S(1)}, bf16[1,8,2304]{2,1,0:T(8,...) custom-call(bf16[1,8,2304]{2,1,0:T(8,128)(2,1)} %refs_0_.1, bf16[1,8,2304]{2,1,0:T(8,128)(2,1)} %refs_1_.1, ...), custom_call_target="tpu_custom_call" | custom-call | tf_op jit(solution)/shard_map/relay/pallas_call | solution.py:537
  83.7 1.6 %results.1 = (bf16[1,8,2304]{2,1,0:T(8,128)(2,1)}, bf16[1,8,2304]{2,1,0:T(8,128)(2,1)}, bf16[1,8,2304]{2,1,0:T(8,128)(2,1)}, bf16[1,8,2304]{2,1,0:T(8,128)(2,1)}...) custom-call(bf16[1,8,2304]{2,1,0:T(8,128)(2,1)S(1)} %get-tuple-element.18.refs_0_, ...), custom_call_target="tpu_custom_call" | custom-call | tf_op jit(solution)/shard_map/results/pallas_call | solution.py:597
